TPU v7x, 32 devices: a whole 2x2x4 slice. The times are simulated.
32 devices in a mesh: scen: 2 (over x), gx: 16 (over z, y, core).
Axes of the slice: x: 2, y: 2, z: 4, core: 2. Of those that a mesh axis runs over, the one named last changes fastest.
Arguments:
- populations: float32 [54, 16, 4, 8, 256], P('scen', 'gx'), parts along dimension 0, may hold values from 0.15 to 2
- cell_kind: int32 [16, 4, 8, 512], P('gx', None, None, 'scen'), parts along dimension 3, may hold values from 0 to 4, as said below
- profile: int32 [16, 4, 8, 512], P('gx', None, None, 'scen'), parts along dimension 3, may hold values from 0 to 7
- vent_table: float32 [16, 3], P('scen'), parts along dimension 0, may hold values from -0.08 to 0.08
- rates: float32 [27], replicated, may hold values from 1 to 1.9
Outputs:
- advanced: float32 [54, 16, 4, 8, 256], P('scen', 'gx'), parts along dimension 0
There are 2 independent parts, one for each index of `scen`. A program takes and returns all parts, laid end to end along the dimension named above; an argument that names none is the same for every part. Nothing has to cross between parts.
Inputs may be any that keep to these rules, and one draw needn't show every extreme that they name: `cell_kind`: 0 fluid, 1 wall, 2 vent, 3 inflow, 4 outflow.
All inputs are finite; a program needn't handle non-finite values.
Results may differ from a plain program's by a relative error of at most 0.0003.
Values sent between devices are 32-bit elements; how exact they have to be, the bound alone decides.
No kernel may reach another device: no remote copies, remote signals or barrier semaphores. Data moves between devices by JAX's collectives and lax.ppermute only.
A program may use at most 64 MiB of HBM per device.

v0:
```python
import functools

import jax
import jax.numpy as jnp
import numpy as np
from jax import lax
from jax.experimental import pallas as pl
from jax.experimental.pallas import tpu as pltpu
from jax.sharding import PartitionSpec as P

PY = 8
STEPS = 3
LANES = 128
OPEN = 1e30
CONSERVED = (0, 9, 3, 1)


def direction(k):
    return k // 9 - 1, k // 3 % 3 - 1, k % 3 - 1


def equilibrium_moments():
    speeds = np.array([direction(k) for k in range(27)], float)
    single = np.array([1.0 / 6.0, 2.0 / 3.0, 1.0 / 6.0])
    weights = np.kron(np.kron(single, single), single)
    powers = np.array([[1.0, 1.0, 1.0], [-1.0, 0.0, 1.0], [1.0, 0.0, 1.0]])
    moments = np.kron(np.kron(powers, powers), powers)
    basis = [np.ones(27)]
    basis += [3.0 * speeds[:, i] for i in range(3)]
    basis += [4.5 * speeds[:, i] ** 2 - 1.5 for i in range(3)]
    basis += [9.0 * speeds[:, i] * speeds[:, j] for i, j in ((0, 1), (0, 2), (1, 2))]
    return 27.0 * moments @ (weights[:, None] * np.stack(basis, 1))


TABLE = equilibrium_moments()


def along_axes(values, change):
    for stride in (9, 3, 1):
        out = list(values)
        for k in range(27):
            if k // stride % 3 == 0:
                trio = (values[k], values[k + stride], values[k + 2 * stride])
                out[k], out[k + stride], out[k + 2 * stride] = change(*trio)
        values = out
    return values


def to_moment(low, mid, high):
    total = low + high
    return total + 4.0 * mid, high - low, total


def from_moment(zeroth, first, second):
    return second - first, 0.5 * (zeroth - second), first + second


def equilibrium_terms(density, velocity):
    ux, uy, uz = velocity
    jx, jy, jz = density * ux, density * uy, density * uz
    terms = (density, jx, jy, jz, jx * ux, jy * uy, jz * uz, jx * uy, jx * uz, jy * uz)
    result = []
    for k in range(27):
        value = None
        for t in range(10):
            coefficient = float(TABLE[k, t])
            if abs(coefficient) > 1e-9:
                piece = terms[t] if abs(coefficient - 1.0) < 1e-9 else coefficient * terms[t]
                value = piece if value is None else value + piece
        result.append(jnp.zeros_like(density) if value is None else value)
    return result


def density_velocity(raw):
    inverse = 1.0 / raw[0]
    return raw[0] * (1.0 / 216.0), (raw[9] * inverse, raw[3] * inverse, raw[1] * inverse)


def vent_velocity(profile, table_ref):
    parts = [jnp.zeros(profile.shape, jnp.float32) for _ in range(3)]
    for p in range(table_ref.shape[0]):
        match = profile == p
        parts = [jnp.where(match, table_ref[p, c], parts[c]) for c in range(3)]
    return parts


def relaxed(raw, equal, rates_ref):
    result = []
    for k in range(27):
        if k in CONSERVED:
            result.append(0.125 * raw[k])
        else:
            rate = rates_ref[k]
            result.append(rate * equal[k] + ((1.0 - rate) * 0.125) * raw[k])
    return result


def tiles(depth, cells, body):
    def plane(x, carry):
        for start in range(0, cells, LANES):
            body(x, slice(start, start + LANES))
        return carry

    lax.fori_loop(0, depth, plane, 0)


def pack(collided, sends, cell_refs):
    send_x, send_up, send_down, corner_up, corner_down = sends
    depth, rows = collided.shape[1], collided.shape[2]
    for side, a, x in ((0, 1, depth - 1), (1, -1, 0)):
        for i in range(9):
            send_x[side, i] = collided[9 * (a + 1) + i, x]
        for i, ref in enumerate(cell_refs):
            send_x[side, 9 + i] = ref[x].astype(jnp.float32)
    for buffer, corner, b, y in ((send_up, corner_up, 1, rows - 1), (send_down, corner_down, -1, 0)):
        for a in (-1, 0, 1):
            for e in (-1, 0, 1):
                k = 9 * (a + 1) + 3 * (b + 1) + e + 1
                first = (3 * (a + 1) + e + 1) * depth
                for x in range(depth):
                    buffer[first + x : first + x + 1, :] = collided[k, x, y : y + 1, :]
        for i, ref in enumerate(cell_refs):
            for x in range(depth):
                at = (9 + i) * depth + x
                buffer[at : at + 1, :] = ref[x, y : y + 1, :].astype(jnp.float32)
        for side, a, x in ((0, 1, depth - 1), (1, -1, 0)):
            for e in (-1, 0, 1):
                k = 9 * (a + 1) + 3 * (b + 1) + e + 1
                corner[side, e + 1 : e + 2, :] = collided[k, x, y : y + 1, :]
            for i, ref in enumerate(cell_refs):
                corner[side, 3 + i : 4 + i, :] = ref[x, y : y + 1, :].astype(jnp.float32)


def first_kernel(populations, kind, profile, rates, collided, *sends):
    depth, cells = populations.shape[1], populations.shape[3]

    def body(x, span):
        raw = along_axes([populations[k, x, :, span] for k in range(27)], to_moment)
        equal = equilibrium_terms(*density_velocity(raw))
        values = along_axes(relaxed(raw, equal, rates), from_moment)
        for k in range(27):
            collided[k, x, :, span] = values[k]

    tiles(depth, cells, body)
    pack(collided, sends, (kind, profile))


def shifted(plane, row, b, e, sublane):
    rows, cells = plane.shape
    if b:
        plane = pltpu.roll(plane, b % rows, 0)
        edge = 0 if b == 1 else rows - 1
        plane = jnp.where(sublane == edge, jnp.broadcast_to(row, plane.shape), plane)
    if e:
        plane = pltpu.roll(plane, e % cells, 1)
    return plane


def cell_fields(kind, profile, table):
    open_cell = (kind == 0) | (kind >= 3)
    vent = kind == 2
    velocity = vent_velocity(profile, table)
    return [jnp.where(open_cell, OPEN, 0.0)] + [jnp.where(vent, 6.0 * v, 0.0) for v in velocity]


def make_fields(halo, kind, profile, table, place, kinds_row, profiles_row, planes, edges):
    recv_x, recv_low, recv_high, corner_low, corner_high = halo
    depth = kind.shape[0]
    for x in range(-1, depth + 1):
        if 0 <= x < depth:
            kinds, profiles = kind[x].astype(jnp.float32), profile[x].astype(jnp.float32)
        else:
            side = 0 if x < 0 else 1
            kinds, profiles = recv_x[side, 9], recv_x[side, 10]
        for c, value in enumerate(cell_fields(kinds, profiles, table)):
            planes[c, x + 1] = value
    row_sides = ((recv_low, corner_low, 0), (recv_high, corner_high, PY - 1))
    for s, (buffer, corner, outer) in enumerate(row_sides):
        for target, i in ((kinds_row, 0), (profiles_row, 1)):
            target[...] = jnp.zeros(target.shape, jnp.float32)
            target[0:1, :] = corner[0, 3 + i : 4 + i, :]
            at = (9 + i) * depth
            for x in range(depth):
                target[x + 1 : x + 2, :] = buffer[at + x : at + x + 1, :]
            target[depth + 1 : depth + 2, :] = corner[1, 3 + i : 4 + i, :]
        kinds = jnp.where(place[0] == outer, 1.0, kinds_row[...])
        for c, value in enumerate(cell_fields(kinds, profiles_row[...], table)):
            edges[s, c] = value


def stream(collided, halo, bounce, passed, fields):
    recv_x, recv_low, recv_high, corner_low, corner_high = halo
    depth, rows, cells = collided.shape[1:]
    sublane = lax.broadcasted_iota(jnp.int32, (rows, cells), 0)
    lane = lax.broadcasted_iota(jnp.int32, (rows, cells), 1)
    for k in range(27):
        a, b, e = direction(k)
        for x in range(depth):
            if k == 13:
                passed[k, x] = collided[k, x]
                continue
            source = x - a
            side = 0 if source < 0 else 1
            inside = 0 <= source < depth
            plane = collided[k, source] if inside else recv_x[side, 3 * (b + 1) + e + 1]
            row = None
            if b:
                buffer, corner = (recv_low, corner_low) if b == 1 else (recv_high, corner_high)
                at = (3 * (a + 1) + e + 1) * depth + source
                row = buffer[at : at + 1, :] if inside else corner[side, e + 1 : e + 2, :]
            if fields is not None:
                planes, edges = fields

                def combine(read):
                    value = read(0)
                    for c, step in enumerate((a, b, e)):
                        if step:
                            value = value + read(c + 1) if step > 0 else value - read(c + 1)
                    return value

                term = combine(lambda c: planes[c, source + 1])
                term_row = None
                if b:
                    s = 0 if b == 1 else 1
                    term_row = combine(lambda c: edges[s, c, source + 1 : source + 2, :])
                term = shifted(term, term_row, b, e, sublane)
                if e:
                    term = jnp.where(lane == (0 if e == 1 else cells - 1), 0.0, term)
                bounce[k, x] = term
            term = bounce[k, x]
            value = shifted(plane, row, b, e, sublane)
            passed[k, x] = jnp.where(term > 0.5 * OPEN, value, collided[26 - k, x] + term)


def chosen(kind, profile, table, velocity):
    vent = vent_velocity(profile, table)
    return [
        jnp.where(kind == 3, vent[c], jnp.where(kind == 4, velocity[c], 0.0)) for c in range(3)
    ]


def collide_cells(passed, kind, profile, table, rates, collided):
    depth, cells = passed.shape[1], passed.shape[3]

    def body(x, span):
        kinds = kind[x, :, span]
        fluid = kinds == 0
        raw = along_axes([passed[k, x, :, span] for k in range(27)], to_moment)
        density, velocity = density_velocity(raw)
        forced = chosen(kinds, profile[x, :, span], table, velocity)
        density = jnp.where(fluid, density, 1.0)
        velocity = [jnp.where(fluid, velocity[c], forced[c]) for c in range(3)]
        equal = equilibrium_terms(density, velocity)
        mixed = relaxed(raw, equal, rates)
        values = [jnp.where(fluid, mixed[k], equal[k]) for k in range(27)]
        values = along_axes(values, from_moment)
        for k in range(27):
            collided[k, x, :, span] = values[k]

    tiles(depth, cells, body)


def finish_cells(passed, kind, profile, table, advanced):
    depth, cells = passed.shape[1], passed.shape[3]

    def body(x, span):
        kinds = kind[x, :, span]
        fluid = kinds == 0
        values = [passed[k, x, :, span] for k in range(27)]
        velocity = density_velocity(along_axes(values, to_moment))[1]
        ux, uy, uz = chosen(kinds, profile[x, :, span], table, velocity)
        base = 1.0 - 1.5 * (ux * ux + uy * uy + uz * uz)
        for k in range(27):
            projected = None
            for step, u in zip(direction(k), (ux, uy, uz)):
                if step:
                    signed = u if step > 0 else -u
                    projected = signed if projected is None else projected + signed
            equal = base if projected is None else base + projected * (3.0 + 4.5 * projected)
            advanced[k, x, :, span] = jnp.where(fluid, values[k], equal)

    tiles(depth, cells, body)


def second_kernel(*refs):
    collided, *halo = refs[:6]
    kind, profile, table, rates, place = refs[6:11]
    out, bounce = refs[11:13]
    sends = refs[13:18]
    passed, kinds_row, profiles_row, planes, edges = refs[18:]
    make_fields(halo, kind, profile, table, place, kinds_row, profiles_row, planes, edges)
    stream(collided, halo, bounce, passed, (planes, edges))
    collide_cells(passed, kind, profile, table, rates, out)
    pack(out, sends, ())


def middle_kernel(*refs):
    collided, *halo = refs[:6]
    bounce, kind, profile, table, rates = refs[6:11]
    out = refs[11]
    sends = refs[12:17]
    passed = refs[17]
    stream(collided, halo, bounce, passed, None)
    collide_cells(passed, kind, profile, table, rates, out)
    pack(out, sends, ())


def last_kernel(*refs):
    collided, *halo = refs[:6]
    bounce, kind, profile, table, advanced, passed = refs[6:]
    stream(collided, halo, bounce, passed, None)
    finish_cells(passed, kind, profile, table, advanced)


def passed_along(value, steps):
    count = lax.axis_size("gx")
    pairs = [(source, (source + steps) % count) for source in range(count)]
    return lax.ppermute(value, "gx", pairs)


def both_sides(value, across):
    if lax.axis_size("gx") == 2 * PY:
        return passed_along(value, PY + across)
    return jnp.stack(
        [passed_along(value[0], PY + across), passed_along(value[1], across - PY)]
    )


def exchange(sends):
    send_x, send_up, send_down, corner_up, corner_down = sends
    return (
        both_sides(send_x, 0),
        passed_along(send_up, 1),
        passed_along(send_down, -1),
        both_sides(corner_up, 1),
        both_sides(corner_down, -1),
    )


def round_up(value, step):
    return -(-value // step) * step


def local(populations, cell_kind, profile, vent_table, rates):
    scaled = populations[:, 0]
    kind, profile = cell_kind[0], profile[0]
    depth, rows, cells = kind.shape
    f32 = jnp.float32
    field = jax.ShapeDtypeStruct(scaled.shape, f32)
    vmem = pl.BlockSpec(memory_space=pltpu.VMEM)
    smem = pl.BlockSpec(memory_space=pltpu.SMEM)
    place = ((lax.axis_index("gx") + PY // 2) % PY).astype(jnp.int32).reshape(1)

    def send_shapes(extra):
        along = jax.ShapeDtypeStruct((round_up((9 + extra) * depth, 8), cells), f32)
        corner = jax.ShapeDtypeStruct((2, 8, cells), f32)
        across = jax.ShapeDtypeStruct((2, 9 + extra, rows, cells), f32)
        return (across, along, along, corner, corner)

    def call(body, specs, outs, scratch, name):
        return pl.pallas_call(
            body,
            in_specs=specs,
            out_specs=jax.tree.map(lambda _: vmem, outs),
            out_shape=outs,
            scratch_shapes=scratch,
            name=name,
        )

    buffer = pltpu.VMEM(scaled.shape, f32)
    edge_rows = round_up(depth + 2, 8)
    collided, *sends = call(
        first_kernel, [vmem] * 3 + [smem], (field,) + send_shapes(2), [], "first"
    )(scaled, kind, profile, rates)
    halo = exchange(sends)
    collided, bounce, *sends = call(
        second_kernel,
        [vmem] * 8 + [smem] * 3,
        (field, field) + send_shapes(0),
        [
            buffer,
            pltpu.VMEM((edge_rows, cells), f32),
            pltpu.VMEM((edge_rows, cells), f32),
            pltpu.VMEM((4, depth + 2, rows, cells), f32),
            pltpu.VMEM((2, 4, edge_rows, cells), f32),
        ],
        "second",
    )(collided, *halo, kind, profile, vent_table, rates, place)
    for _ in range(STEPS - 2):
        halo = exchange(sends)
        collided, *sends = call(
            middle_kernel,
            [vmem] * 9 + [smem] * 2,
            (field,) + send_shapes(0),
            [buffer],
            "middle",
        )(collided, *halo, bounce, kind, profile, vent_table, rates)
    halo = exchange(sends)
    advanced = call(last_kernel, [vmem] * 9 + [smem], field, [buffer], "last")(
        collided, *halo, bounce, kind, profile, vent_table
    )
    return advanced[:, None]


def solution(mesh):
    return jax.shard_map(
        local,
        mesh=mesh,
        in_specs=(
            P("scen", "gx", None, None, None),
            P("gx", None, None, "scen"),
            P("gx", None, None, "scen"),
            P("scen", None),
            P(),
        ),
        out_specs=P("scen", "gx", None, None, None),
        check_vma=False,
    )
```

profile of v0, /device:TPU:1, one launch (start us, length us, event | category | flops | bytes accessed | tf_op | source)
XLA Modules:
  0.0 53.4 jit_solution(13934762015227075623)
XLA Ops:
  0.0 2.7 %first.1 = (f32[27,4,8,256]{3,2,1,0:T(8,128)}, f32[2,11,8,256]{3,2,1,0:T(8,128)}, f32[48,256]{1,0:T(8,128)}, f32[48,256]{1,0:T(8,128)}, f32[2,8,256]{2,1,0:T(8,128)}, /*index=5*/f32[2,8,256]{2,1,0:T(8,128)}) custom-call(f32[27,4,8,256]{3,2,1,0:T(8,128)} %bitcast.7, s32[4,8,256]{2,1,0:T(8,128)} %bitcast.8, s32[4,8,256]{2,1,0:T(8,128)} %bitcast.12, f32[27]{0:T(128)} %refs_10_.1), custom_call_target="tpu_custom_call" | custom-call | tf_op jit(solution)/shard_map/first/pallas_call | solution.py:372
  2.7 3.1 %collective-permute-start = (f32[2,11,8,256]{3,2,1,0:T(8,128)}, f32[2,11,8,256]{3,2,1,0:T(8,128)S(1)}, u32[]{:S(2)}, u32[]{:S(2)}) collective-permute-start(f32[2,11,8,256]{3,2,1,0:T(8,128)} %get-tuple-element.25), channel_id=1, source_target_pairs={{0,8},{1,9},{2,10},{3,11},{4,12},{5,13},{6,14},{7,15},{8,0},{9,1},... | collective-permute-start | bytes 540680 | tf_op jit(solution)/shard_map/ppermute | solution.py:318
  5.8 2.1 %collective-permute-start.1 = (f32[48,256]{1,0:T(8,128)}, f32[48,256]{1,0:T(8,128)S(1)}, u32[]{:S(2)}, u32[]{:S(2)}) collective-permute-start(f32[48,256]{1,0:T(8,128)} %get-tuple-element.26), channel_id=1, source_target_pairs={{0,1},{1,2},{2,3},{3,4},{4,5},{5,6},{6,7},{7,8},{8,9},{9,10},{10,1... | collective-permute-start | bytes 147464 | tf_op jit(solution)/shard_map/ppermute | solution.py:318
  7.9 1.5 %collective-permute-start.3 = (f32[2,8,256]{2,1,0:T(8,128)}, f32[2,8,256]{2,1,0:T(8,128)S(1)}, u32[]{:S(2)}, u32[]{:S(2)}) collective-permute-start(f32[2,8,256]{2,1,0:T(8,128)} %get-tuple-element.28), channel_id=1, source_target_pairs={{0,9},{1,10},{2,11},{3,12},{4,13},{5,14},{6,15},{7,0},{8,1},{9,2},... | collective-permute-start | bytes 49160 | tf_op jit(solution)/shard_map/ppermute | solution.py:318
  9.4 1.1 %collective-permute-start.4 = (f32[2,8,256]{2,1,0:T(8,128)}, f32[2,8,256]{2,1,0:T(8,128)S(1)}, u32[]{:S(2)}, u32[]{:S(2)}) collective-permute-start(f32[2,8,256]{2,1,0:T(8,128)} %get-tuple-element.29), channel_id=1, source_target_pairs={{0,7},{1,8},{2,9},{3,10},{4,11},{5,12},{6,13},{7,14},{8,15},{9,0},... | collective-permute-start | bytes 49160 | tf_op jit(solution)/shard_map/ppermute | solution.py:318
  10.5 0.7 %copy-done.15 = f32[8,3]{0,1:T(4,128)S(1)} copy-done((f32[8,3]{0,1:T(4,128)S(1)}, f32[8,3]{0,1:T(4,128)}, u32[]{:S(2)}) %copy-start.15) | copy-done | bytes 120
  11.2 0.7 %copy.6.refs_8_.refs_9_ = f32[8,3]{1,0:T(8,128)} copy(f32[8,3]{0,1:T(4,128)S(1)} %copy-done.15) | data formatting | bytes 192 | tf_op args[3]
  11.9 4.4 %collective-permute-done.3.refs_4_ = f32[2,8,256]{2,1,0:T(8,128)S(1)} collective-permute-done((f32[2,8,256]{2,1,0:T(8,128)}, f32[2,8,256]{2,1,0:T(8,128)S(1)}, u32[]{:S(2)}, u32[]{:S(2)}) %collective-permute-start.3) | collective-permute-done | bytes 16416 | tf_op jit(solution)/shard_map/ppermute | solution.py:318
  16.3 1.2 %collective-permute-done.4.refs_5_ = f32[2,8,256]{2,1,0:T(8,128)S(1)} collective-permute-done((f32[2,8,256]{2,1,0:T(8,128)}, f32[2,8,256]{2,1,0:T(8,128)S(1)}, u32[]{:S(2)}, u32[]{:S(2)}) %collective-permute-start.4) | collective-permute-done | bytes 16416 | tf_op jit(solution)/shard_map/ppermute | solution.py:318
  17.5 0.5 %copy-done.10 = f32[2,8,256]{2,1,0:T(8,128)} copy-done((f32[2,8,256]{2,1,0:T(8,128)}, f32[2,8,256]{2,1,0:T(8,128)S(1)}, u32[]{:S(2)}) %copy-start.10) | copy-done | bytes 16408
  18.2 3.7 %second.1 = (f32[27,4,8,256]{3,2,1,0:T(8,128)}, f32[27,4,8,256]{3,2,1,0:T(8,128)}, f32[2,9,8,256]{3,2,1,0:T(8,128)}, f32[40,256]{1,0:T(8,128)}, f32[40,256]{1,0:...) custom-call(f32[27,4,8,256]{3,2,1,0:T(8,128)} %get-tuple-element.24.refs_0_, f32[2,11,8,256]{3,2,1,0:T(8,128)} %copy-done, ...), custom_call_target="tpu_custom_call" | custom-call | tf_op jit(solution)/shard_map/second/pallas_call | solution.py:376
  22.4 2.6 %collective-permute-start.7 = (f32[40,256]{1,0:T(8,128)}, f32[40,256]{1,0:T(8,128)S(1)}, u32[]{:S(2)}, u32[]{:S(2)}) collective-permute-start(f32[40,256]{1,0:T(8,128)} %get-tuple-element.33), channel_id=1, source_target_pairs={{0,15},{1,0},{2,1},{3,2},{4,3},{5,4},{6,5},{7,6},{8,7},{9,8},{10,9... | collective-permute-start | bytes 122888 | tf_op jit(solution)/shard_map/ppermute | solution.py:318
  25.0 1.5 %collective-permute-start.8 = (f32[2,8,256]{2,1,0:T(8,128)}, f32[2,8,256]{2,1,0:T(8,128)S(1)}, u32[]{:S(2)}, u32[]{:S(2)}) collective-permute-start(f32[2,8,256]{2,1,0:T(8,128)} %get-tuple-element.34), channel_id=1, source_target_pairs={{0,9},{1,10},{2,11},{3,12},{4,13},{5,14},{6,15},{7,0},{8,1},{9,2},... | collective-permute-start | bytes 49160 | tf_op jit(solution)/shard_map/ppermute | solution.py:318
  26.4 1.2 %collective-permute-start.9 = (f32[2,8,256]{2,1,0:T(8,128)}, f32[2,8,256]{2,1,0:T(8,128)S(1)}, u32[]{:S(2)}, u32[]{:S(2)}) collective-permute-start(f32[2,8,256]{2,1,0:T(8,128)} %get-tuple-element.35), channel_id=1, source_target_pairs={{0,7},{1,8},{2,9},{3,10},{4,11},{5,12},{6,13},{7,14},{8,15},{9,0},... | collective-permute-start | bytes 49160 | tf_op jit(solution)/shard_map/ppermute | solution.py:318
  27.6 5.9 %collective-permute-done.8.refs_4_ = f32[2,8,256]{2,1,0:T(8,128)S(1)} collective-permute-done((f32[2,8,256]{2,1,0:T(8,128)}, f32[2,8,256]{2,1,0:T(8,128)S(1)}, u32[]{:S(2)}, u32[]{:S(2)}) %collective-permute-start.8) | collective-permute-done | bytes 16416 | tf_op jit(solution)/shard_map/ppermute | solution.py:318
  33.5 0.5 copy-done.11
  34.2 3.5 %middle.1 = (f32[27,4,8,256]{3,2,1,0:T(8,128)}, f32[2,9,8,256]{3,2,1,0:T(8,128)}, f32[40,256]{1,0:T(8,128)}, f32[40,256]{1,0:T(8,128)}, f32[2,8,256]{2,1,0:T(8,128)}, /*index=5*/f32[2,8,256]{2,1,0:T(8,128)}) custom-call(f32[27,4,8,256]{3,2,1,0:T(8,128)} %get-tuple-element.30.refs_0_, f32[2,9,8,256]{3,2,1,0:T(8,128)} %copy-done.1, f32[40,256]{1,0:T(8,128)} %copy-done.5, ...), custom_call_target="tpu_custom_call" | custom-call | tf_op jit(solution)/shard_map/middle/pallas_call | solution.py:391
  38.1 0.6 %collective-permute-start.12 = (f32[40,256]{1,0:T(8,128)}, f32[40,256]{1,0:T(8,128)S(1)}, u32[]{:S(2)}, u32[]{:S(2)}) collective-permute-start(f32[40,256]{1,0:T(8,128)} %get-tuple-element.40), channel_id=1, source_target_pairs={{0,15},{1,0},{2,1},{3,2},{4,3},{5,4},{6,5},{7,6},{8,7},{9,8},{10,9... | collective-permute-start | bytes 122888 | tf_op jit(solution)/shard_map/ppermute | solution.py:318
  38.7 3.4 %collective-permute-start.13 = (f32[2,8,256]{2,1,0:T(8,128)}, f32[2,8,256]{2,1,0:T(8,128)S(1)}, u32[]{:S(2)}, u32[]{:S(2)}) collective-permute-start(f32[2,8,256]{2,1,0:T(8,128)} %get-tuple-element.41), channel_id=1, source_target_pairs={{0,9},{1,10},{2,11},{3,12},{4,13},{5,14},{6,15},{7,0},{8,1},{9,2},... | collective-permute-start | bytes 49160 | tf_op jit(solution)/shard_map/ppermute | solution.py:318
  42.1 1.2 %collective-permute-start.14 = (f32[2,8,256]{2,1,0:T(8,128)}, f32[2,8,256]{2,1,0:T(8,128)S(1)}, u32[]{:S(2)}, u32[]{:S(2)}) collective-permute-start(f32[2,8,256]{2,1,0:T(8,128)} %get-tuple-element.42), channel_id=1, source_target_pairs={{0,7},{1,8},{2,9},{3,10},{4,11},{5,12},{6,13},{7,14},{8,15},{9,0},... | collective-permute-start | bytes 49160 | tf_op jit(solution)/shard_map/ppermute | solution.py:318
  43.3 5.4 %collective-permute-done.13.refs_4_ = f32[2,8,256]{2,1,0:T(8,128)S(1)} collective-permute-done((f32[2,8,256]{2,1,0:T(8,128)}, f32[2,8,256]{2,1,0:T(8,128)S(1)}, u32[]{:S(2)}, u32[]{:S(2)}) %collective-permute-start.13) | collective-permute-done | bytes 16416 | tf_op jit(solution)/shard_map/ppermute | solution.py:318
  48.6 0.9 %collective-permute-done.14.refs_5_ = f32[2,8,256]{2,1,0:T(8,128)S(1)} collective-permute-done((f32[2,8,256]{2,1,0:T(8,128)}, f32[2,8,256]{2,1,0:T(8,128)S(1)}, u32[]{:S(2)}, u32[]{:S(2)}) %collective-permute-start.14) | collective-permute-done | bytes 16416 | tf_op jit(solution)/shard_map/ppermute | solution.py:318
  49.6 0.5 %copy-done.14 = f32[2,8,256]{2,1,0:T(8,128)} copy-done((f32[2,8,256]{2,1,0:T(8,128)}, f32[2,8,256]{2,1,0:T(8,128)S(1)}, u32[]{:S(2)}) %copy-start.14) | copy-done | bytes 16408
  50.3 3.2 %last.1 = f32[27,4,8,256]{3,2,1,0:T(8,128)} custom-call(f32[27,4,8,256]{3,2,1,0:T(8,128)} %get-tuple-element.37.refs_0_, f32[2,9,8,256]{3,2,1,0:T(8,128)} %copy-done.2, f32[40,256]{1,0:T(8,128)} %copy-done.7, f32[40,256]{1,0:T(8,128)} %copy-done.8, f32[2,8,256]{2,1,0:T(8,128)} %copy-done.13, f32[2,8,256]{2,1,0:T(8,128)} %copy-done.14, ...), custom_call_target="tpu_custom_call" | custom-call | tf_op jit(solution)/shard_map/last/pallas_call | solution.py:399
  (43 shorter events, 1.3 us)
Async XLA Ops:
  2.7 14.8 %collective-permute-start = (f32[2,11,8,256]{3,2,1,0:T(8,128)}, f32[2,11,8,256]{3,2,1,0:T(8,128)S(1)}, u32[]{:S(2)}, u32[]{:S(2)}) collective-permute-start(f32[2,11,8,256]{3,2,1,0:T(8,128)} %get-tuple-element.25), channel_id=1, source_target_pairs={{0,8},{1,9},{2,10},{3,11},{4,12},{5,13},{6,14},{7,15},{8,0},{9,1},... | collective-permute-start | bytes 540680 | tf_op jit(solution)/shard_map/ppermute | solution.py:318
  5.8 11.7 %collective-permute-start.1 = (f32[48,256]{1,0:T(8,128)}, f32[48,256]{1,0:T(8,128)S(1)}, u32[]{:S(2)}, u32[]{:S(2)}) collective-permute-start(f32[48,256]{1,0:T(8,128)} %get-tuple-element.26), channel_id=1, source_target_pairs={{0,1},{1,2},{2,3},{3,4},{4,5},{5,6},{6,7},{7,8},{8,9},{9,10},{10,1... | collective-permute-start | bytes 147464 | tf_op jit(solution)/shard_map/ppermute | solution.py:318
  7.9 9.6 %collective-permute-start.2 = (f32[48,256]{1,0:T(8,128)}, f32[48,256]{1,0:T(8,128)S(1)}, u32[]{:S(2)}, u32[]{:S(2)}) collective-permute-start(f32[48,256]{1,0:T(8,128)} %get-tuple-element.27), channel_id=1, source_target_pairs={{0,15},{1,0},{2,1},{3,2},{4,3},{5,4},{6,5},{7,6},{8,7},{9,8},{10,9... | collective-permute-start | bytes 147464 | tf_op jit(solution)/shard_map/ppermute | solution.py:318
  7.9 8.4 %collective-permute-start.3 = (f32[2,8,256]{2,1,0:T(8,128)}, f32[2,8,256]{2,1,0:T(8,128)S(1)}, u32[]{:S(2)}, u32[]{:S(2)}) collective-permute-start(f32[2,8,256]{2,1,0:T(8,128)} %get-tuple-element.28), channel_id=1, source_target_pairs={{0,9},{1,10},{2,11},{3,12},{4,13},{5,14},{6,15},{7,0},{8,1},{9,2},... | collective-permute-start | bytes 49160 | tf_op jit(solution)/shard_map/ppermute | solution.py:318
  9.4 8.1 %collective-permute-start.4 = (f32[2,8,256]{2,1,0:T(8,128)}, f32[2,8,256]{2,1,0:T(8,128)S(1)}, u32[]{:S(2)}, u32[]{:S(2)}) collective-permute-start(f32[2,8,256]{2,1,0:T(8,128)} %get-tuple-element.29), channel_id=1, source_target_pairs={{0,7},{1,8},{2,9},{3,10},{4,11},{5,12},{6,13},{7,14},{8,15},{9,0},... | collective-permute-start | bytes 49160 | tf_op jit(solution)/shard_map/ppermute | solution.py:318
  10.5 0.7 %copy-start.15 = (f32[8,3]{0,1:T(4,128)S(1)}, f32[8,3]{0,1:T(4,128)}, u32[]{:S(2)}) copy-start(f32[8,3]{0,1:T(4,128)} %param.8) | copy-start | bytes 292
  16.3 1.2 %copy-start.9 = (f32[2,8,256]{2,1,0:T(8,128)}, f32[2,8,256]{2,1,0:T(8,128)S(1)}, u32[]{:S(2)}) copy-start(f32[2,8,256]{2,1,0:T(8,128)S(1)} %collective-permute-done.3.refs_4_) | copy-start | bytes 49156
  17.4 0.6 %copy-start.3 = (f32[48,256]{1,0:T(8,128)}, f32[48,256]{1,0:T(8,128)S(1)}, u32[]{:S(2)}) copy-start(f32[48,256]{1,0:T(8,128)S(1)} %collective-permute-done.1.refs_2_) | copy-start | bytes 147460
  17.5 0.6 %copy-start.4 = (f32[48,256]{1,0:T(8,128)}, f32[48,256]{1,0:T(8,128)S(1)}, u32[]{:S(2)}) copy-start(f32[48,256]{1,0:T(8,128)S(1)} %collective-permute-done.2.refs_3_) | copy-start | bytes 147460
  17.5 0.7 %copy-start = (f32[2,11,8,256]{3,2,1,0:T(8,128)}, f32[2,11,8,256]{3,2,1,0:T(8,128)S(1)}, u32[]{:S(2)}) copy-start(f32[2,11,8,256]{3,2,1,0:T(8,128)S(1)} %collective-permute-done.refs_1_) | copy-start | bytes 540676
  21.9 11.7 %collective-permute-start.5 = (f32[2,9,8,256]{3,2,1,0:T(8,128)}, f32[2,9,8,256]{3,2,1,0:T(8,128)S(1)}, u32[]{:S(2)}, u32[]{:S(2)}) collective-permute-start(f32[2,9,8,256]{3,2,1,0:T(8,128)} %get-tuple-element.31), channel_id=1, source_target_pairs={{0,8},{1,9},{2,10},{3,11},{4,12},{5,13},{6,14},{7,15},{8,0},{9,1},... | collective-permute-start | bytes 442376 | tf_op jit(solution)/shard_map/ppermute | solution.py:318
  21.9 11.6 %collective-permute-start.6 = (f32[40,256]{1,0:T(8,128)}, f32[40,256]{1,0:T(8,128)S(1)}, u32[]{:S(2)}, u32[]{:S(2)}) collective-permute-start(f32[40,256]{1,0:T(8,128)} %get-tuple-element.32), channel_id=1, source_target_pairs={{0,1},{1,2},{2,3},{3,4},{4,5},{5,6},{6,7},{7,8},{8,9},{9,10},{10,1... | collective-permute-start | bytes 122888 | tf_op jit(solution)/shard_map/ppermute | solution.py:318
  22.4 11.1 %collective-permute-start.7 = (f32[40,256]{1,0:T(8,128)}, f32[40,256]{1,0:T(8,128)S(1)}, u32[]{:S(2)}, u32[]{:S(2)}) collective-permute-start(f32[40,256]{1,0:T(8,128)} %get-tuple-element.33), channel_id=1, source_target_pairs={{0,15},{1,0},{2,1},{3,2},{4,3},{5,4},{6,5},{7,6},{8,7},{9,8},{10,9... | collective-permute-start | bytes 122888 | tf_op jit(solution)/shard_map/ppermute | solution.py:318
  25.0 8.5 %collective-permute-start.8 = (f32[2,8,256]{2,1,0:T(8,128)}, f32[2,8,256]{2,1,0:T(8,128)S(1)}, u32[]{:S(2)}, u32[]{:S(2)}) collective-permute-start(f32[2,8,256]{2,1,0:T(8,128)} %get-tuple-element.34), channel_id=1, source_target_pairs={{0,9},{1,10},{2,11},{3,12},{4,13},{5,14},{6,15},{7,0},{8,1},{9,2},... | collective-permute-start | bytes 49160 | tf_op jit(solution)/shard_map/ppermute | solution.py:318
  26.4 7.0 %collective-permute-start.9 = (f32[2,8,256]{2,1,0:T(8,128)}, f32[2,8,256]{2,1,0:T(8,128)S(1)}, u32[]{:S(2)}, u32[]{:S(2)}) collective-permute-start(f32[2,8,256]{2,1,0:T(8,128)} %get-tuple-element.35), channel_id=1, source_target_pairs={{0,7},{1,8},{2,9},{3,10},{4,11},{5,12},{6,13},{7,14},{8,15},{9,0},... | collective-permute-start | bytes 49160 | tf_op jit(solution)/shard_map/ppermute | solution.py:318
  33.5 0.7 %copy-start.1 = (f32[2,9,8,256]{3,2,1,0:T(8,128)}, f32[2,9,8,256]{3,2,1,0:T(8,128)S(1)}, u32[]{:S(2)}) copy-start(f32[2,9,8,256]{3,2,1,0:T(8,128)S(1)} %collective-permute-done.5.refs_1_) | copy-start | bytes 442372
  37.7 11.9 %collective-permute-start.10 = (f32[2,9,8,256]{3,2,1,0:T(8,128)}, f32[2,9,8,256]{3,2,1,0:T(8,128)S(1)}, u32[]{:S(2)}, u32[]{:S(2)}) collective-permute-start(f32[2,9,8,256]{3,2,1,0:T(8,128)} %get-tuple-element.38), channel_id=1, source_target_pairs={{0,8},{1,9},{2,10},{3,11},{4,12},{5,13},{6,14},{7,15},{8,0},{9,1},... | collective-permute-start | bytes 442376 | tf_op jit(solution)/shard_map/ppermute | solution.py:318
  38.1 11.5 %collective-permute-start.11 = (f32[40,256]{1,0:T(8,128)}, f32[40,256]{1,0:T(8,128)S(1)}, u32[]{:S(2)}, u32[]{:S(2)}) collective-permute-start(f32[40,256]{1,0:T(8,128)} %get-tuple-element.39), channel_id=1, source_target_pairs={{0,1},{1,2},{2,3},{3,4},{4,5},{5,6},{6,7},{7,8},{8,9},{9,10},{10,1... | collective-permute-start | bytes 122888 | tf_op jit(solution)/shard_map/ppermute | solution.py:318
  38.1 11.5 %collective-permute-start.12 = (f32[40,256]{1,0:T(8,128)}, f32[40,256]{1,0:T(8,128)S(1)}, u32[]{:S(2)}, u32[]{:S(2)}) collective-permute-start(f32[40,256]{1,0:T(8,128)} %get-tuple-element.40), channel_id=1, source_target_pairs={{0,15},{1,0},{2,1},{3,2},{4,3},{5,4},{6,5},{7,6},{8,7},{9,8},{10,9... | collective-permute-start | bytes 122888 | tf_op jit(solution)/shard_map/ppermute | solution.py:318
  38.7 9.9 %collective-permute-start.13 = (f32[2,8,256]{2,1,0:T(8,128)}, f32[2,8,256]{2,1,0:T(8,128)S(1)}, u32[]{:S(2)}, u32[]{:S(2)}) collective-permute-start(f32[2,8,256]{2,1,0:T(8,128)} %get-tuple-element.41), channel_id=1, source_target_pairs={{0,9},{1,10},{2,11},{3,12},{4,13},{5,14},{6,15},{7,0},{8,1},{9,2},... | collective-permute-start | bytes 49160 | tf_op jit(solution)/shard_map/ppermute | solution.py:318
  42.1 7.5 %collective-permute-start.14 = (f32[2,8,256]{2,1,0:T(8,128)}, f32[2,8,256]{2,1,0:T(8,128)S(1)}, u32[]{:S(2)}, u32[]{:S(2)}) collective-permute-start(f32[2,8,256]{2,1,0:T(8,128)} %get-tuple-element.42), channel_id=1, source_target_pairs={{0,7},{1,8},{2,9},{3,10},{4,11},{5,12},{6,13},{7,14},{8,15},{9,0},... | collective-permute-start | bytes 49160 | tf_op jit(solution)/shard_map/ppermute | solution.py:318
  48.6 1.0 %copy-start.13 = (f32[2,8,256]{2,1,0:T(8,128)}, f32[2,8,256]{2,1,0:T(8,128)S(1)}, u32[]{:S(2)}) copy-start(f32[2,8,256]{2,1,0:T(8,128)S(1)} %collective-permute-done.13.refs_4_) | copy-start | bytes 49156
  49.6 0.6 %copy-start.8 = (f32[40,256]{1,0:T(8,128)}, f32[40,256]{1,0:T(8,128)S(1)}, u32[]{:S(2)}) copy-start(f32[40,256]{1,0:T(8,128)S(1)} %collective-permute-done.12.refs_3_) | copy-start | bytes 122884
  49.6 0.7 %copy-start.2 = (f32[2,9,8,256]{3,2,1,0:T(8,128)}, f32[2,9,8,256]{3,2,1,0:T(8,128)S(1)}, u32[]{:S(2)}) copy-start(f32[2,9,8,256]{3,2,1,0:T(8,128)S(1)} %collective-permute-done.10.refs_1_) | copy-start | bytes 442372
  (7 other events, 4.2 us)
where the time goes:
time: 53.7 us; the launch traced here: 53.4 us
  starting transfers between devices  19.2 us (36%)
  waiting for transfers between devices  17.7 us (33%)
  Pallas kernels  13 us (24%)
  local copies, waits for them, and re-layouts  3.35 us (6%)
    ppermute x15, starting transfers between devices, passed_along(): return lax.ppermute(value, 'gx', pairs)  19.2 us
    ppermute x15, waiting for transfers between devices, passed_along(): return lax.ppermute(value, 'gx', pairs)  17.7 us
    pallas_call x1, Pallas kernels, local(): call(second_kernel, [vmem] * 8 + [smem] * 3, (field, field) + send_shapes...  3.69 us
    pallas_call x1, Pallas kernels, local(): call(middle_kernel, [vmem] * 9 + [smem] * 2, (field,) + send_shapes(0), [...  3.48 us
    unnamed x33, local copies, waits for them, and re-layouts  3.35 us
    pallas_call x1, Pallas kernels, local(): call(last_kernel, [vmem] * 9 + [smem], field, [buffer], 'last')  3.16 us
    pallas_call x1, Pallas kernels, local(): call(first_kernel, [vmem] * 3 + [smem], (field,) + send_shapes(2), [], 'f...  2.66 us
  transfers between devices with their start and end apart: 15, of which 5 were waited for; matrix products, arithmetic and copies ran while one was open for 1% of the time, Pallas kernels for 0%

commit v1 on v0

v1 whole, which is shorter than its diff:
```python
import functools

import jax
import jax.numpy as jnp
import numpy as np
from jax import lax
from jax.experimental import pallas as pl
from jax.experimental.pallas import tpu as pltpu
from jax.sharding import PartitionSpec as P

PY = 8
STEPS = 3
LANES = 128
OPEN = 1e30
CONSERVED = (0, 9, 3, 1)


def direction(k):
    return k // 9 - 1, k // 3 % 3 - 1, k % 3 - 1


def equilibrium_moments():
    speeds = np.array([direction(k) for k in range(27)], float)
    single = np.array([1.0 / 6.0, 2.0 / 3.0, 1.0 / 6.0])
    weights = np.kron(np.kron(single, single), single)
    powers = np.array([[1.0, 1.0, 1.0], [-1.0, 0.0, 1.0], [1.0, 0.0, 1.0]])
    moments = np.kron(np.kron(powers, powers), powers)
    basis = [np.ones(27)]
    basis += [3.0 * speeds[:, i] for i in range(3)]
    basis += [4.5 * speeds[:, i] ** 2 - 1.5 for i in range(3)]
    basis += [9.0 * speeds[:, i] * speeds[:, j] for i, j in ((0, 1), (0, 2), (1, 2))]
    return 27.0 * moments @ (weights[:, None] * np.stack(basis, 1))


TABLE = equilibrium_moments()


def along_axes(values, change):
    for stride in (9, 3, 1):
        out = list(values)
        for k in range(27):
            if k // stride % 3 == 0:
                trio = (values[k], values[k + stride], values[k + 2 * stride])
                out[k], out[k + stride], out[k + 2 * stride] = change(*trio)
        values = out
    return values


def to_moment(low, mid, high):
    total = low + high
    return total + 4.0 * mid, high - low, total


def from_moment(zeroth, first, second):
    return second - first, 0.5 * (zeroth - second), first + second


def equilibrium_terms(density, velocity):
    ux, uy, uz = velocity
    jx, jy, jz = density * ux, density * uy, density * uz
    terms = (density, jx, jy, jz, jx * ux, jy * uy, jz * uz, jx * uy, jx * uz, jy * uz)
    result = []
    for k in range(27):
        value = None
        for t in range(10):
            coefficient = float(TABLE[k, t])
            if abs(coefficient) > 1e-9:
                piece = terms[t] if abs(coefficient - 1.0) < 1e-9 else coefficient * terms[t]
                value = piece if value is None else value + piece
        result.append(jnp.zeros_like(density) if value is None else value)
    return result


def density_velocity(raw):
    inverse = 1.0 / raw[0]
    return raw[0] * (1.0 / 216.0), (raw[9] * inverse, raw[3] * inverse, raw[1] * inverse)


def vent_velocity(profile, table_ref):
    parts = [jnp.zeros(profile.shape, jnp.float32) for _ in range(3)]
    for p in range(table_ref.shape[0]):
        match = profile == p
        parts = [jnp.where(match, table_ref[p, c], parts[c]) for c in range(3)]
    return parts


def relaxed(raw, equal, rates_ref):
    result = []
    for k in range(27):
        if k in CONSERVED:
            result.append(0.125 * raw[k])
        else:
            rate = rates_ref[k]
            result.append(rate * equal[k] + ((1.0 - rate) * 0.125) * raw[k])
    return result


def tiles(depth, cells, body):
    def plane(x, carry):
        for start in range(0, cells, LANES):
            body(x, slice(start, start + LANES))
        return carry

    lax.fori_loop(0, depth, plane, 0)


class Planes:
    def __init__(self, edge, inner):
        self.edge, self.inner = edge, inner
        self.depth = inner.shape[1] + 2

    def __getitem__(self, index):
        k, x = index[0], index[1]
        rest = tuple(index[2:])
        if x == 0:
            return self.edge[(k, 0) + rest]
        if x == self.depth - 1:
            return self.edge[(k, 1) + rest]
        return self.inner[(k, x - 1) + rest]


def pack_x(edge, send_x, cell_refs):
    for side, a, at in ((0, 1, 1), (1, -1, 0)):
        for i in range(9):
            send_x[side, i] = edge[9 * (a + 1) + i, at]
        for i, ref in enumerate(cell_refs):
            send_x[side, 9 + i] = ref[(ref.shape[0] - 1) * at].astype(jnp.float32)


def pack_y(field, rows, sends, faces, place, cell_refs):
    depth = field.depth
    for buffer, b, y in ((faces[0], 1, rows - 1), (faces[1], -1, 0)):
        for a in (-1, 0, 1):
            for e in (-1, 0, 1):
                k = 9 * (a + 1) + 3 * (b + 1) + e + 1
                first = (3 * (a + 1) + e + 1) * depth
                for x in range(depth):
                    buffer[first + x : first + x + 1, :] = field[k, x, slice(y, y + 1), slice(None)]
        for i, ref in enumerate(cell_refs):
            for x in range(depth):
                at = (9 + i) * depth + x
                buffer[at : at + 1, :] = ref[x, y : y + 1, :].astype(jnp.float32)
    even = place[1] == 0

    @pl.when(even)
    def _():
        sends[0][...] = faces[0][...]
        sends[1][...] = faces[1][...]

    @pl.when(jnp.logical_not(even))
    def _():
        sends[0][...] = faces[1][...]
        sends[1][...] = faces[0][...]


def unpack_y(pairs, corner, low, high, corner_low, corner_high, place):
    even = place[1] == 0

    def take(first, second):
        first[0][...] = pairs[0][...]
        second[0][...] = pairs[1][...]
        if corner is not None:
            for side in range(2):
                first[1][side] = corner[side, 0:8, :]
                second[1][side] = corner[side, 8:16, :]

    @pl.when(even)
    def _():
        take((high, corner_high), (low, corner_low))

    @pl.when(jnp.logical_not(even))
    def _():
        take((low, corner_low), (high, corner_high))


def corner_kernel(first, second, out, *, depth, extra):
    for side, a, x in ((0, 1, depth - 1), (1, -1, 0)):
        for p, ref in enumerate((first, second)):
            for e in range(3):
                at = (3 * (a + 1) + e) * depth + x
                out[side, 8 * p + e : 8 * p + e + 1, :] = ref[at : at + 1, :]
            for i in range(extra):
                at = (9 + i) * depth + x
                out[side, 8 * p + 3 + i : 8 * p + 4 + i, :] = ref[at : at + 1, :]


def collide_all(source, rates, target):
    def body(x, span):
        raw = along_axes([source[k, x, :, span] for k in range(27)], to_moment)
        equal = equilibrium_terms(*density_velocity(raw))
        values = along_axes(relaxed(raw, equal, rates), from_moment)
        for k in range(27):
            target[k, x, :, span] = values[k]

    return body


def first_edge_kernel(populations, kind, profile, rates, edge, send_x):
    body = collide_all(populations, rates, edge)
    for start in range(0, populations.shape[3], LANES):
        body(0, slice(start, start + LANES))
    base = 18 * pl.program_id(0)
    for i in range(9):
        send_x[0, i] = edge[base + i, 0]
    send_x[0, 9] = kind[0].astype(jnp.float32)
    send_x[0, 10] = profile[0].astype(jnp.float32)


def first_inner_kernel(populations, edge, kind, profile, rates, place, inner, *rest):
    sends, faces = rest[:2], rest[2:]
    depth, rows, cells = populations.shape[1:]

    def plane(x, carry):
        for start in range(0, cells, LANES):
            span = slice(start, start + LANES)
            raw = along_axes([populations[k, x + 1, :, span] for k in range(27)], to_moment)
            equal = equilibrium_terms(*density_velocity(raw))
            values = along_axes(relaxed(raw, equal, rates), from_moment)
            for k in range(27):
                inner[k, x, :, span] = values[k]
        return carry

    lax.fori_loop(0, depth - 2, plane, 0)
    pack_y(Planes(edge, inner), rows, sends, faces, place, (kind, profile))


def shifted(plane, row, b, e, sublane):
    rows, cells = plane.shape
    if b:
        plane = pltpu.roll(plane, b % rows, 0)
        edge = 0 if b == 1 else rows - 1
        plane = jnp.where(sublane == edge, jnp.broadcast_to(row, plane.shape), plane)
    if e:
        plane = pltpu.roll(plane, e % cells, 1)
    return plane


def cell_fields(kind, profile, table):
    open_cell = (kind == 0) | (kind >= 3)
    vent = kind == 2
    velocity = vent_velocity(profile, table)
    return [jnp.where(open_cell, OPEN, 0.0)] + [jnp.where(vent, 6.0 * v, 0.0) for v in velocity]


def make_fields(halo, kind, profile, table, place, kinds_row, profiles_row, planes, edges, span):
    recv_x, recv_low, recv_high, corner_low, corner_high = halo
    depth = kind.shape[0]
    for x in span:
        if 0 <= x < depth:
            kinds, profiles = kind[x].astype(jnp.float32), profile[x].astype(jnp.float32)
        else:
            side = 0 if x < 0 else 1
            kinds, profiles = recv_x[side, 9], recv_x[side, 10]
        for c, value in enumerate(cell_fields(kinds, profiles, table)):
            planes[c, x + 1] = value
    row_sides = ((recv_low, corner_low, 0), (recv_high, corner_high, PY - 1))
    for s, (buffer, corner, outer) in enumerate(row_sides):
        for target, i in ((kinds_row, 0), (profiles_row, 1)):
            target[...] = jnp.zeros(target.shape, jnp.float32)
            at = (9 + i) * depth
            for x in range(depth):
                target[x + 1 : x + 2, :] = buffer[at + x : at + x + 1, :]
            if -1 in span:
                target[0:1, :] = corner[0, 3 + i : 4 + i, :]
                target[depth + 1 : depth + 2, :] = corner[1, 3 + i : 4 + i, :]
        kinds = jnp.where(place[0] == outer, 1.0, kinds_row[...])
        for c, value in enumerate(cell_fields(kinds, profiles_row[...], table)):
            edges[s, c] = value


def stream(field, halo, bounce, passed, fields, targets, shape):
    recv_x, recv_low, recv_high, corner_low, corner_high = halo
    depth, rows, cells = shape
    sublane = lax.broadcasted_iota(jnp.int32, (rows, cells), 0)
    lane = lax.broadcasted_iota(jnp.int32, (rows, cells), 1)
    for k in range(27):
        a, b, e = direction(k)
        for at_x, x in enumerate(targets):
            if k == 13:
                passed[k, at_x] = field[k, x]
                continue
            source = x - a
            side = 0 if source < 0 else 1
            inside = 0 <= source < depth
            plane = field[k, source] if inside else recv_x[side, 3 * (b + 1) + e + 1]
            row = None
            if b:
                buffer, corner = (recv_low, corner_low) if b == 1 else (recv_high, corner_high)
                at = (3 * (a + 1) + e + 1) * depth + source
                row = buffer[at : at + 1, :] if inside else corner[side, e + 1 : e + 2, :]
            if fields is not None:
                planes, edges = fields

                def combine(read):
                    value = read(0)
                    for c, step in enumerate((a, b, e)):
                        if step:
                            value = value + read(c + 1) if step > 0 else value - read(c + 1)
                    return value

                term = combine(lambda c: planes[c, source + 1])
                term_row = None
                if b:
                    s = 0 if b == 1 else 1
                    term_row = combine(lambda c: edges[s, c, source + 1 : source + 2, :])
                term = shifted(term, term_row, b, e, sublane)
                if e:
                    term = jnp.where(lane == (0 if e == 1 else cells - 1), 0.0, term)
                bounce[k, at_x] = term
            term = bounce[k, at_x]
            value = shifted(plane, row, b, e, sublane)
            passed[k, at_x] = jnp.where(term > 0.5 * OPEN, value, field[26 - k, x] + term)


def chosen(kind, profile, table, velocity):
    vent = vent_velocity(profile, table)
    return [
        jnp.where(kind == 3, vent[c], jnp.where(kind == 4, velocity[c], 0.0)) for c in range(3)
    ]


def collide_cells(passed, kind, profile, table, rates, collided, base, stride):
    count, cells = passed.shape[1], passed.shape[3]

    def body(x, span):
        kinds = kind[base + x * stride, :, span]
        fluid = kinds == 0
        raw = along_axes([passed[k, x, :, span] for k in range(27)], to_moment)
        density, velocity = density_velocity(raw)
        forced = chosen(kinds, profile[base + x * stride, :, span], table, velocity)
        density = jnp.where(fluid, density, 1.0)
        velocity = [jnp.where(fluid, velocity[c], forced[c]) for c in range(3)]
        equal = equilibrium_terms(density, velocity)
        mixed = relaxed(raw, equal, rates)
        values = [jnp.where(fluid, mixed[k], equal[k]) for k in range(27)]
        values = along_axes(values, from_moment)
        for k in range(27):
            collided[k, x, :, span] = values[k]

    tiles(count, cells, body)


def finish_cells(passed, kind, profile, table, advanced, base, stride, out_base, out_stride):
    count, cells = passed.shape[1], passed.shape[3]

    def body(x, span):
        kinds = kind[base + x * stride, :, span]
        fluid = kinds == 0
        values = [passed[k, x, :, span] for k in range(27)]
        velocity = density_velocity(along_axes(values, to_moment))[1]
        ux, uy, uz = chosen(kinds, profile[base + x * stride, :, span], table, velocity)
        rest = 1.0 - 1.5 * (ux * ux + uy * uy + uz * uz)
        for k in range(27):
            projected = None
            for step, u in zip(direction(k), (ux, uy, uz)):
                if step:
                    signed = u if step > 0 else -u
                    projected = signed if projected is None else projected + signed
            equal = rest if projected is None else rest + projected * (3.0 + 4.5 * projected)
            advanced[k, out_base + x * out_stride, :, span] = jnp.where(fluid, values[k], equal)

    tiles(count, cells, body)


def inner_kernel(*refs, fresh, last):
    refs = list(refs)
    edge, inner, first, second = refs[:4]
    del refs[:4]
    bounce = None if fresh else refs.pop(0)
    kind, profile, table, rates, place, out = refs[:6]
    del refs[:6]
    if fresh:
        bounce = refs.pop(0)
    passed, low, high = refs[:3]
    depth, rows, cells = kind.shape
    unpack_y((first, second), None, low, high, None, None, place)
    halo = (None, low, high, None, None)
    fields = None
    if fresh:
        kinds_row, profiles_row, planes, edges = refs[3:]
        make_fields(
            halo, kind, profile, table, place, kinds_row, profiles_row, planes, edges, range(depth)
        )
        fields = (planes, edges)
    targets = range(1, depth - 1)
    stream(Planes(edge, inner), halo, bounce, passed, fields, targets, kind.shape)
    if last:
        finish_cells(passed, kind, profile, table, out, 1, 1, 0, 1)
    else:
        collide_cells(passed, kind, profile, table, rates, out, 1, 1)


def edge_kernel(*refs, fresh, last):
    refs = list(refs)
    edge, inner, next_inner, recv_x, first, second, corner = refs[:7]
    del refs[:7]
    bounce = None if fresh else refs.pop(0)
    kind, profile, table, rates, place, out = refs[:6]
    del refs[:6]
    if fresh:
        bounce = refs.pop(0)
    if not last:
        send_x, send_first, send_second = refs[:3]
        del refs[:3]
    passed, low, high, corner_low, corner_high = refs[:5]
    del refs[:5]
    depth, rows, cells = kind.shape
    unpack_y((first, second), corner, low, high, corner_low, corner_high, place)
    halo = (recv_x, low, high, corner_low, corner_high)
    fields = None
    if fresh:
        kinds_row, profiles_row, planes, edges = refs[:4]
        del refs[:4]
        make_fields(
            halo, kind, profile, table, place, kinds_row, profiles_row, planes, edges,
            range(-1, depth + 1),
        )
        fields = (planes, edges)
    targets = (0, depth - 1)
    stream(Planes(edge, inner), halo, bounce, passed, fields, targets, kind.shape)
    if last:
        finish_cells(passed, kind, profile, table, out, 0, depth - 1, 0, depth - 1)
        for k in range(27):
            for x in range(1, depth - 1):
                out[k, x] = next_inner[k, x - 1]
        return
    collide_cells(passed, kind, profile, table, rates, out, 0, depth - 1)
    pack_x(out, send_x, ())
    pack_y(Planes(out, next_inner), rows, (send_first, send_second), refs, place, ())


def passed_along(value, steps):
    count = lax.axis_size("gx")
    pairs = [(source, (source + steps) % count) for source in range(count)]
    return lax.ppermute(value, "gx", pairs)


def swapped(value, parity):
    count = lax.axis_size("gx")
    pairs = []
    for source in range(parity, count, 2):
        target = (source + 1) % count
        if (target + PY // 2) % PY:
            pairs += [(source, target), (target, source)]
    return lax.ppermute(value, "gx", pairs)


def both_sides(value):
    if lax.axis_size("gx") == 2 * PY:
        return passed_along(value, PY)
    return jnp.stack([passed_along(value[0], PY), passed_along(value[1], -PY)])


def round_up(value, step):
    return -(-value // step) * step


def local(populations, cell_kind, profile, vent_table, rates):
    scaled = populations[:, 0]
    kind, profile = cell_kind[0], profile[0]
    depth, rows, cells = kind.shape
    f32 = jnp.float32
    vmem = pl.BlockSpec(memory_space=pltpu.VMEM)
    smem = pl.BlockSpec(memory_space=pltpu.SMEM)
    index = lax.axis_index("gx")
    place = jnp.stack([(index + PY // 2) % PY, index % 2]).astype(jnp.int32)

    def array(*shape):
        return jax.ShapeDtypeStruct(shape, f32)

    def scratch(*shape):
        return pltpu.VMEM(shape, f32)

    def call(body, specs, outs, scratch_shapes, name, **options):
        return pl.pallas_call(
            functools.partial(body, **options) if options else body,
            in_specs=specs,
            out_specs=jax.tree.map(lambda _: vmem, outs),
            out_shape=outs,
            scratch_shapes=scratch_shapes,
            name=name,
        )

    edge_shape, inner_shape = (27, 2, rows, cells), (27, depth - 2, rows, cells)
    wide = (round_up(11 * depth, 8), cells)
    narrow = (round_up(9 * depth, 8), cells)
    line = round_up(depth + 2, 8)
    field_scratch = [
        scratch(line, cells),
        scratch(line, cells),
        scratch(4, depth + 2, rows, cells),
        scratch(2, 4, line, cells),
    ]
    corners = [scratch(2, 8, cells)] * 2

    plane_at = lambda i: (i * (depth - 1), 0, 0)
    edge, send_x = pl.pallas_call(
        first_edge_kernel,
        grid=(2,),
        in_specs=[
            pl.BlockSpec((27, 1, rows, cells), lambda i: (0, i * (depth - 1), 0, 0)),
            pl.BlockSpec((1, rows, cells), plane_at),
            pl.BlockSpec((1, rows, cells), plane_at),
            smem,
        ],
        out_specs=(
            pl.BlockSpec((27, 1, rows, cells), lambda i: (0, i, 0, 0)),
            pl.BlockSpec((1, 11, rows, cells), lambda i: (1 - i, 0, 0, 0)),
        ),
        out_shape=(array(*edge_shape), array(2, 11, rows, cells)),
        name="first_edge",
    )(scaled, kind, profile, rates)
    recv_x = both_sides(send_x)
    inner, *sends = call(
        first_inner_kernel,
        [vmem] * 4 + [smem] * 2,
        (array(*inner_shape), array(*wide), array(*wide)),
        [scratch(*wide)] * 2,
        "first_inner",
    )(scaled, edge, kind, profile, rates, place)
    shared = (kind, profile, vent_table, rates, place)
    shared_specs = [vmem] * 2 + [smem] * 3
    inner_bounce = edge_bounce = None
    for step in range(STEPS):
        fresh, last = step == 0, step == STEPS - 1
        extra = 2 if fresh else 0
        shape = wide if fresh else narrow
        pairs = swapped(sends[0], 0), swapped(sends[1], 1)
        corner = call(
            corner_kernel, [vmem] * 2, array(2, 16, cells), [], "corner", depth=depth, extra=extra
        )(*pairs)
        corner = both_sides(corner)
        outs = [array(*inner_shape)] + ([array(*inner_shape)] if fresh else [])
        known = () if fresh else (inner_bounce,)
        results = call(
            inner_kernel,
            [vmem] * (4 + len(known)) + shared_specs,
            tuple(outs),
            [scratch(*inner_shape)] + [scratch(*shape)] * 2 + (field_scratch if fresh else []),
            "inner",
            fresh=fresh,
            last=last,
        )(edge, inner, *pairs, *known, *shared)
        next_inner = results[0]
        if fresh:
            inner_bounce = results[1]
        outs = [array(27, depth, rows, cells) if last else array(*edge_shape)]
        outs += [array(*edge_shape)] if fresh else []
        outs += [] if last else [array(2, 9, rows, cells), array(*narrow), array(*narrow)]
        known = () if fresh else (edge_bounce,)
        results = list(
            call(
                edge_kernel,
                [vmem] * (7 + len(known)) + shared_specs,
                tuple(outs),
                [scratch(*edge_shape)]
                + [scratch(*shape)] * 2
                + corners
                + (field_scratch if fresh else [])
                + ([] if last else [scratch(*narrow)] * 2),
                "edge",
                fresh=fresh,
                last=last,
            )(edge, inner, next_inner, recv_x, *pairs, corner, *known, *shared)
        )
        edge = results.pop(0)
        inner = next_inner
        if fresh:
            edge_bounce = results.pop(0)
        if not last:
            recv_x = both_sides(results.pop(0))
            sends = results
    return edge[:, None]


def solution(mesh):
    return jax.shard_map(
        local,
        mesh=mesh,
        in_specs=(
            P("scen", "gx", None, None, None),
            P("gx", None, None, "scen"),
            P("gx", None, None, "scen"),
            P("scen", None),
            P(),
        ),
        out_specs=P("scen", "gx", None, None, None),
        check_vma=False,
    )
```

time: 53.7 us -> 70.6 us (1.31)
  the two profiles are of different devices: /device:TPU:1 before, /device:TPU:0 now
where the time goes in v1:
time: 70.6 us; the launch traced here: 70 us
  Pallas kernels  25.3 us (36%)
  waiting for transfers between devices  20 us (28%)
  starting transfers between devices  18.8 us (27%)
  local copies, waits for them, and re-layouts  5.14 us (7%)
    ppermute x6, waiting for transfers between devices, swapped(): return lax.ppermute(value, 'gx', pairs)  14.6 us
    ppermute x6, starting transfers between devices, swapped(): return lax.ppermute(value, 'gx', pairs)  10.2 us
    pallas_call x3, Pallas kernels, local(): call(edge_kernel, [vmem] * (7 + len(known)) + shared_specs, tuple(outs),...  8.91 us
    ppermute x6, starting transfers between devices, passed_along(): return lax.ppermute(value, 'gx', pairs)  8.65 us
    pallas_call x3, Pallas kernels, local(): call(inner_kernel, [vmem] * (4 + len(known)) + shared_specs, tuple(outs),...  7.75 us
    ppermute x6, waiting for transfers between devices, passed_along(): return lax.ppermute(value, 'gx', pairs)  5.4 us
    unnamed x27, local copies, waits for them, and re-layouts  5.14 us
    pallas_call x3, Pallas kernels, local(): call(corner_kernel, [vmem] * 2, array(2, 16, cells), [], 'corner', depth=...  4.28 us
  transfers between devices with their start and end apart: 12, of which 5 were waited for; matrix products, arithmetic and copies ran while one was open for 2% of the time, Pallas kernels for 21%

profile of v1, /device:TPU:0, one launch (start us, length us, event | category | flops | bytes accessed | tf_op | source)
XLA Modules:
  0.0 70.0 jit_solution(3184121083585892448)
XLA Ops:
  0.0 2.0 %first_edge.1 = (f32[27,2,8,256]{3,2,1,0:T(8,128)}, f32[2,11,8,256]{3,2,1,0:T(8,128)}) custom-call(f32[27,4,8,256]{3,2,1,0:T(8,128)} %bitcast.8, s32[4,8,256]{2,1,0:T(8,128)} %bitcast.10, s32[4,8,256]{2,1,0:T(8,128)} %bitcast.18, f32[27]{0:T(128)} %refs_11_.3), custom_call_target="tpu_custom_call" | custom-call | tf_op jit(solution)/shard_map/first_edge/pallas_call | solution.py:497
  2.0 4.1 %collective-permute-start.2 = (f32[2,11,8,256]{3,2,1,0:T(8,128)}, f32[2,11,8,256]{3,2,1,0:T(8,128)S(1)}, u32[]{:S(2)}, u32[]{:S(2)}) collective-permute-start(f32[2,11,8,256]{3,2,1,0:T(8,128)} %get-tuple-element.26), channel_id=1, source_target_pairs={{0,8},{1,9},{2,10},{3,11},{4,12},{5,13},{6,14},{7,15},{8,0},{9,1},... | collective-permute-start | bytes 540680 | tf_op jit(solution)/shard_map/ppermute | solution.py:435
  6.6 2.4 %first_inner.1 = (f32[27,2,8,256]{3,2,1,0:T(8,128)}, f32[48,256]{1,0:T(8,128)}, f32[48,256]{1,0:T(8,128)}) custom-call(f32[27,4,8,256]{3,2,1,0:T(8,128)} %bitcast.9, f32[27,2,8,256]{3,2,1,0:T(8,128)} %get-tuple-element.21.edge.refs_0_, s32[4,8,256]{2,1,0:T(8,128)} %bitcast.11, s32[4,8,256]{2,1,0:T(8,128)} %bitcast.19, f32[27]{0:T(128)} %refs_11_.3, ...), custom_call_target="tpu_custom_call" | custom-call | tf_op jit(solution)/shard_map/first_inner/pallas_call | solution.py:514
  9.0 4.4 %collective-permute-start.1 = (f32[48,256]{1,0:T(8,128)}, f32[48,256]{1,0:T(8,128)S(1)}, u32[]{:S(2)}, u32[]{:S(2)}) collective-permute-start(f32[48,256]{1,0:T(8,128)} %get-tuple-element.24), channel_id=1, source_target_pairs={{1,2},{2,1},{5,6},{6,5},{7,8},{8,7},{9,10},{10,9},{13,14},{14,13},... | collective-permute-start | bytes 147464 | tf_op jit(solution)/shard_map/ppermute | solution.py:445
  13.5 3.8 %collective-permute-done.1.refs_3_.second.refs_5_ = f32[48,256]{1,0:T(8,128)S(1)} collective-permute-done((f32[48,256]{1,0:T(8,128)}, f32[48,256]{1,0:T(8,128)S(1)}, u32[]{:S(2)}, u32[]{:S(2)}) %collective-permute-start.1) | collective-permute-done | bytes 49184 | tf_op jit(solution)/shard_map/ppermute | solution.py:445
  18.0 1.4 %corner.3 = f32[2,16,256]{2,1,0:T(8,128)} custom-call(f32[48,256]{1,0:T(8,128)} %copy-done, f32[48,256]{1,0:T(8,128)} %copy-done.1), custom_call_target="tpu_custom_call" | custom-call | tf_op jit(solution)/shard_map/corner/pallas_call | solution.py:529
  19.4 1.8 %collective-permute-start.3 = (f32[2,16,256]{2,1,0:T(8,128)}, f32[2,16,256]{2,1,0:T(8,128)S(1)}, u32[]{:S(2)}, u32[]{:S(2)}) collective-permute-start(f32[2,16,256]{2,1,0:T(8,128)} %corner.3), channel_id=1, source_target_pairs={{0,8},{1,9},{2,10},{3,11},{4,12},{5,13},{6,14},{7,15},{8,0},{9,1},... | collective-permute-start | bytes 98312 | tf_op jit(solution)/shard_map/ppermute | solution.py:435
  21.2 0.7 copy.6.refs_6_.refs_9_.refs_7_.refs_10_
  21.9 2.7 %inner.3 = (f32[27,2,8,256]{3,2,1,0:T(8,128)}, f32[27,2,8,256]{3,2,1,0:T(8,128)}) custom-call(f32[27,2,8,256]{3,2,1,0:T(8,128)} %get-tuple-element.21.edge.refs_0_, f32[27,2,8,256]{3,2,1,0:T(8,128)} %get-tuple-element.22.refs_1_, f32[48,256]{1,0:T(8,128)} %copy-done, f32[48,256]{1,0:T(8,128)} %copy-done.1, s32[4,8,256]{2,1,0:T(8,128)} %bitcast.12, ...), custom_call_target="tpu_custom_call" | custom-call | tf_op jit(solution)/shard_map/inner/pallas_call | solution.py:535
  25.2 3.1 %edge.3 = (f32[27,2,8,256]{3,2,1,0:T(8,128)}, f32[27,2,8,256]{3,2,1,0:T(8,128)}, f32[2,9,8,256]{3,2,1,0:T(8,128)}, f32[40,256]{1,0:T(8,128)}, f32[40,256]{1,0:T(8,128)}) custom-call(f32[27,2,8,256]{3,2,1,0:T(8,128)} %get-tuple-element.21.edge.refs_0_, f32[27,2,8,256]{3,2,1,0:T(8,128)} %get-tuple-element.22.refs_1_, ...), custom_call_target="tpu_custom_call" | custom-call | tf_op jit(solution)/shard_map/edge/pallas_call | solution.py:552
  28.4 1.7 %collective-permute-start.6 = (f32[2,9,8,256]{3,2,1,0:T(8,128)}, f32[2,9,8,256]{3,2,1,0:T(8,128)S(1)}, u32[]{:S(2)}, u32[]{:S(2)}) collective-permute-start(f32[2,9,8,256]{3,2,1,0:T(8,128)} %get-tuple-element.31), channel_id=1, source_target_pairs={{0,8},{1,9},{2,10},{3,11},{4,12},{5,13},{6,14},{7,15},{8,0},{9,1},... | collective-permute-start | bytes 442376 | tf_op jit(solution)/shard_map/ppermute | solution.py:435
  30.1 3.4 %collective-permute-start.5 = (f32[40,256]{1,0:T(8,128)}, f32[40,256]{1,0:T(8,128)S(1)}, u32[]{:S(2)}, u32[]{:S(2)}) collective-permute-start(f32[40,256]{1,0:T(8,128)} %get-tuple-element.29), channel_id=1, source_target_pairs={{1,2},{2,1},{5,6},{6,5},{7,8},{8,7},{9,10},{10,9},{13,14},{14,13},... | collective-permute-start | bytes 122888 | tf_op jit(solution)/shard_map/ppermute | solution.py:445
  33.5 4.8 %collective-permute-done.5.refs_3_.second.refs_5_ = f32[40,256]{1,0:T(8,128)S(1)} collective-permute-done((f32[40,256]{1,0:T(8,128)}, f32[40,256]{1,0:T(8,128)S(1)}, u32[]{:S(2)}, u32[]{:S(2)}) %collective-permute-start.5) | collective-permute-done | bytes 40992 | tf_op jit(solution)/shard_map/ppermute | solution.py:445
  38.9 1.4 %corner.4 = f32[2,16,256]{2,1,0:T(8,128)} custom-call(f32[40,256]{1,0:T(8,128)} %copy-done.4, f32[40,256]{1,0:T(8,128)} %copy-done.5), custom_call_target="tpu_custom_call" | custom-call | tf_op jit(solution)/shard_map/corner/pallas_call | solution.py:529
  40.3 2.6 %inner.4.refs_2_.refs_1_ = f32[27,2,8,256]{3,2,1,0:T(8,128)} custom-call(f32[27,2,8,256]{3,2,1,0:T(8,128)} %get-tuple-element.27.refs_0_, f32[27,2,8,256]{3,2,1,0:T(8,128)} %get-tuple-element.25.refs_2_.refs_1_, f32[40,256]{1,0:T(8,128)} %copy-done.4, f32[40,256]{1,0:T(8,128)} %copy-done.5, f32[27,2,8,256]{3,2,1,0:T(8,128)} %get-tuple-element.30.refs_4_, ...), custom_call_target="tpu_custom_call" | custom-call | tf_op jit(solution)/shard_map/inner/pallas_call | solution.py:535
  42.9 4.0 %collective-permute-done.7.refs_6_ = f32[2,16,256]{2,1,0:T(8,128)S(1)} collective-permute-done((f32[2,16,256]{2,1,0:T(8,128)}, f32[2,16,256]{2,1,0:T(8,128)S(1)}, u32[]{:S(2)}, u32[]{:S(2)}) %collective-permute-start.7) | collective-permute-done | bytes 32800 | tf_op jit(solution)/shard_map/ppermute | solution.py:435
  47.6 2.9 %edge.4 = (f32[27,2,8,256]{3,2,1,0:T(8,128)}, f32[2,9,8,256]{3,2,1,0:T(8,128)}, f32[40,256]{1,0:T(8,128)}, f32[40,256]{1,0:T(8,128)}) custom-call(f32[27,2,8,256]{3,2,1,0:T(8,128)} %get-tuple-element.27.refs_0_, f32[27,2,8,256]{3,2,1,0:T(8,128)} %get-tuple-element.25.refs_2_.refs_1_, f32[27,2,8,256]{3,2,1,0:T(8,128)} %inner.4.refs_2_.refs_1_, ...), custom_call_target="tpu_custom_call" | custom-call | tf_op jit(solution)/shard_map/edge/pallas_call | solution.py:552
  50.6 2.3 %collective-permute-start.9 = (f32[40,256]{1,0:T(8,128)}, f32[40,256]{1,0:T(8,128)S(1)}, u32[]{:S(2)}, u32[]{:S(2)}) collective-permute-start(f32[40,256]{1,0:T(8,128)} %get-tuple-element.35), channel_id=1, source_target_pairs={{1,2},{2,1},{5,6},{6,5},{7,8},{8,7},{9,10},{10,9},{13,14},{14,13},... | collective-permute-start | bytes 122888 | tf_op jit(solution)/shard_map/ppermute | solution.py:445
  52.9 5.9 %collective-permute-done.9.refs_3_.second.refs_5_ = f32[40,256]{1,0:T(8,128)S(1)} collective-permute-done((f32[40,256]{1,0:T(8,128)}, f32[40,256]{1,0:T(8,128)S(1)}, u32[]{:S(2)}, u32[]{:S(2)}) %collective-permute-start.9) | collective-permute-done | bytes 40992 | tf_op jit(solution)/shard_map/ppermute | solution.py:445
  59.4 1.4 %corner.5 = f32[2,16,256]{2,1,0:T(8,128)} custom-call(f32[40,256]{1,0:T(8,128)} %copy-done.2, f32[40,256]{1,0:T(8,128)} %copy-done.3), custom_call_target="tpu_custom_call" | custom-call | tf_op jit(solution)/shard_map/corner/pallas_call | solution.py:529
  60.8 1.1 %collective-permute-start.11 = (f32[2,16,256]{2,1,0:T(8,128)}, f32[2,16,256]{2,1,0:T(8,128)S(1)}, u32[]{:S(2)}, u32[]{:S(2)}) collective-permute-start(f32[2,16,256]{2,1,0:T(8,128)} %corner.5), channel_id=1, source_target_pairs={{0,8},{1,9},{2,10},{3,11},{4,12},{5,13},{6,14},{7,15},{8,0},{9,1},... | collective-permute-start | bytes 98312 | tf_op jit(solution)/shard_map/ppermute | solution.py:435
  62.0 2.5 %inner.5.refs_2_ = f32[27,2,8,256]{3,2,1,0:T(8,128)} custom-call(f32[27,2,8,256]{3,2,1,0:T(8,128)} %get-tuple-element.33.refs_0_, f32[27,2,8,256]{3,2,1,0:T(8,128)} %inner.4.refs_2_.refs_1_, f32[40,256]{1,0:T(8,128)} %copy-done.2, f32[40,256]{1,0:T(8,128)} %copy-done.3, f32[27,2,8,256]{3,2,1,0:T(8,128)} %get-tuple-element.30.refs_4_, s32[4,8,256]{2,1,0:T(8,128)} %bitcast.16, ...), custom_call_target="tpu_custom_call" | custom-call | tf_op jit(solution)/shard_map/inner/pallas_call | solution.py:535
  64.5 1.4 %collective-permute-done.11.refs_6_ = f32[2,16,256]{2,1,0:T(8,128)S(1)} collective-permute-done((f32[2,16,256]{2,1,0:T(8,128)}, f32[2,16,256]{2,1,0:T(8,128)S(1)}, u32[]{:S(2)}, u32[]{:S(2)}) %collective-permute-start.11) | collective-permute-done | bytes 32800 | tf_op jit(solution)/shard_map/ppermute | solution.py:435
  67.1 2.8 %edge.5 = f32[27,4,8,256]{3,2,1,0:T(8,128)} custom-call(f32[27,2,8,256]{3,2,1,0:T(8,128)} %get-tuple-element.33.refs_0_, f32[27,2,8,256]{3,2,1,0:T(8,128)} %inner.4.refs_2_.refs_1_, f32[27,2,8,256]{3,2,1,0:T(8,128)} %inner.5.refs_2_, f32[2,9,8,256]{3,2,1,0:T(8,128)} %copy-done.7, f32[40,256]{1,0:T(8,128)} %copy-done.2, f32[40,256]{1,0:T(8,128)} %copy-done.3, ...), custom_call_target="tpu_custom_call" | custom-call | tf_op jit(solution)/shard_map/edge/pallas_call | solution.py:552
  (39 shorter events, 5.1 us)
Async XLA Ops:
  2.0 22.6 %collective-permute-start.2 = (f32[2,11,8,256]{3,2,1,0:T(8,128)}, f32[2,11,8,256]{3,2,1,0:T(8,128)S(1)}, u32[]{:S(2)}, u32[]{:S(2)}) collective-permute-start(f32[2,11,8,256]{3,2,1,0:T(8,128)} %get-tuple-element.26), channel_id=1, source_target_pairs={{0,8},{1,9},{2,10},{3,11},{4,12},{5,13},{6,14},{7,15},{8,0},{9,1},... | collective-permute-start | bytes 540680 | tf_op jit(solution)/shard_map/ppermute | solution.py:435
  9.0 4.5 %collective-permute-start = (f32[48,256]{1,0:T(8,128)}, f32[48,256]{1,0:T(8,128)S(1)}, u32[]{:S(2)}, u32[]{:S(2)}) collective-permute-start(f32[48,256]{1,0:T(8,128)} %get-tuple-element.23), channel_id=1, source_target_pairs={{0,1},{1,0},{2,3},{3,2},{4,5},{5,4},{6,7},{7,6},{8,9},{9,8},{10,11... | collective-permute-start | bytes 147464 | tf_op jit(solution)/shard_map/ppermute | solution.py:445
  9.0 12.2 %copy-start.12 = (f32[8,3]{0,1:T(4,128)S(1)}, f32[8,3]{0,1:T(4,128)}, u32[]{:S(2)}) copy-start(f32[8,3]{0,1:T(4,128)} %param.8) | copy-start | bytes 292
  9.0 8.3 %collective-permute-start.1 = (f32[48,256]{1,0:T(8,128)}, f32[48,256]{1,0:T(8,128)S(1)}, u32[]{:S(2)}, u32[]{:S(2)}) collective-permute-start(f32[48,256]{1,0:T(8,128)} %get-tuple-element.24), channel_id=1, source_target_pairs={{1,2},{2,1},{5,6},{6,5},{7,8},{8,7},{9,10},{10,9},{13,14},{14,13},... | collective-permute-start | bytes 147464 | tf_op jit(solution)/shard_map/ppermute | solution.py:445
  13.5 3.9 %copy-start = (f32[48,256]{1,0:T(8,128)}, f32[48,256]{1,0:T(8,128)S(1)}, u32[]{:S(2)}) copy-start(f32[48,256]{1,0:T(8,128)S(1)} %collective-permute-done.refs_2_.first.refs_4_) | copy-start | bytes 147460
  17.3 0.6 copy-start.1
  19.4 5.1 %collective-permute-start.3 = (f32[2,16,256]{2,1,0:T(8,128)}, f32[2,16,256]{2,1,0:T(8,128)S(1)}, u32[]{:S(2)}, u32[]{:S(2)}) collective-permute-start(f32[2,16,256]{2,1,0:T(8,128)} %corner.3), channel_id=1, source_target_pairs={{0,8},{1,9},{2,10},{3,11},{4,12},{5,13},{6,14},{7,15},{8,0},{9,1},... | collective-permute-start | bytes 98312 | tf_op jit(solution)/shard_map/ppermute | solution.py:435
  24.5 0.6 copy-start.10
  24.6 0.7 copy-start.6
  28.4 18.5 %collective-permute-start.6 = (f32[2,9,8,256]{3,2,1,0:T(8,128)}, f32[2,9,8,256]{3,2,1,0:T(8,128)S(1)}, u32[]{:S(2)}, u32[]{:S(2)}) collective-permute-start(f32[2,9,8,256]{3,2,1,0:T(8,128)} %get-tuple-element.31), channel_id=1, source_target_pairs={{0,8},{1,9},{2,10},{3,11},{4,12},{5,13},{6,14},{7,15},{8,0},{9,1},... | collective-permute-start | bytes 442376 | tf_op jit(solution)/shard_map/ppermute | solution.py:435
  30.1 3.4 %collective-permute-start.4 = (f32[40,256]{1,0:T(8,128)}, f32[40,256]{1,0:T(8,128)S(1)}, u32[]{:S(2)}, u32[]{:S(2)}) collective-permute-start(f32[40,256]{1,0:T(8,128)} %get-tuple-element.28), channel_id=1, source_target_pairs={{0,1},{1,0},{2,3},{3,2},{4,5},{5,4},{6,7},{7,6},{8,9},{9,8},{10,11... | collective-permute-start | bytes 122888 | tf_op jit(solution)/shard_map/ppermute | solution.py:445
  30.1 8.2 %collective-permute-start.5 = (f32[40,256]{1,0:T(8,128)}, f32[40,256]{1,0:T(8,128)S(1)}, u32[]{:S(2)}, u32[]{:S(2)}) collective-permute-start(f32[40,256]{1,0:T(8,128)} %get-tuple-element.29), channel_id=1, source_target_pairs={{1,2},{2,1},{5,6},{6,5},{7,8},{8,7},{9,10},{10,9},{13,14},{14,13},... | collective-permute-start | bytes 122888 | tf_op jit(solution)/shard_map/ppermute | solution.py:445
  33.5 4.8 %copy-start.4 = (f32[40,256]{1,0:T(8,128)}, f32[40,256]{1,0:T(8,128)S(1)}, u32[]{:S(2)}) copy-start(f32[40,256]{1,0:T(8,128)S(1)} %collective-permute-done.4.refs_2_.first.refs_4_) | copy-start | bytes 122884
  38.3 0.6 copy-start.5
  40.3 6.6 %collective-permute-start.7 = (f32[2,16,256]{2,1,0:T(8,128)}, f32[2,16,256]{2,1,0:T(8,128)S(1)}, u32[]{:S(2)}, u32[]{:S(2)}) collective-permute-start(f32[2,16,256]{2,1,0:T(8,128)} %corner.4), channel_id=1, source_target_pairs={{0,8},{1,9},{2,10},{3,11},{4,12},{5,13},{6,14},{7,15},{8,0},{9,1},... | collective-permute-start | bytes 98312 | tf_op jit(solution)/shard_map/ppermute | solution.py:435
  46.9 0.6 copy-start.11
  46.9 0.7 copy-start.8
  50.5 15.4 %collective-permute-start.10 = (f32[2,9,8,256]{3,2,1,0:T(8,128)}, f32[2,9,8,256]{3,2,1,0:T(8,128)S(1)}, u32[]{:S(2)}, u32[]{:S(2)}) collective-permute-start(f32[2,9,8,256]{3,2,1,0:T(8,128)} %get-tuple-element.36), channel_id=1, source_target_pairs={{0,8},{1,9},{2,10},{3,11},{4,12},{5,13},{6,14},{7,15},{8,0},{9,1},... | collective-permute-start | bytes 442376 | tf_op jit(solution)/shard_map/ppermute | solution.py:435
  50.5 2.4 %collective-permute-start.8 = (f32[40,256]{1,0:T(8,128)}, f32[40,256]{1,0:T(8,128)S(1)}, u32[]{:S(2)}, u32[]{:S(2)}) collective-permute-start(f32[40,256]{1,0:T(8,128)} %get-tuple-element.34), channel_id=1, source_target_pairs={{0,1},{1,0},{2,3},{3,2},{4,5},{5,4},{6,7},{7,6},{8,9},{9,8},{10,11... | collective-permute-start | bytes 122888 | tf_op jit(solution)/shard_map/ppermute | solution.py:445
  50.6 8.2 %collective-permute-start.9 = (f32[40,256]{1,0:T(8,128)}, f32[40,256]{1,0:T(8,128)S(1)}, u32[]{:S(2)}, u32[]{:S(2)}) collective-permute-start(f32[40,256]{1,0:T(8,128)} %get-tuple-element.35), channel_id=1, source_target_pairs={{1,2},{2,1},{5,6},{6,5},{7,8},{8,7},{9,10},{10,9},{13,14},{14,13},... | collective-permute-start | bytes 122888 | tf_op jit(solution)/shard_map/ppermute | solution.py:445
  52.9 5.9 %copy-start.2 = (f32[40,256]{1,0:T(8,128)}, f32[40,256]{1,0:T(8,128)S(1)}, u32[]{:S(2)}) copy-start(f32[40,256]{1,0:T(8,128)S(1)} %collective-permute-done.8.refs_2_.first.refs_4_) | copy-start | bytes 122884
  60.8 5.0 %collective-permute-start.11 = (f32[2,16,256]{2,1,0:T(8,128)}, f32[2,16,256]{2,1,0:T(8,128)S(1)}, u32[]{:S(2)}, u32[]{:S(2)}) collective-permute-start(f32[2,16,256]{2,1,0:T(8,128)} %corner.5), channel_id=1, source_target_pairs={{0,8},{1,9},{2,10},{3,11},{4,12},{5,13},{6,14},{7,15},{8,0},{9,1},... | collective-permute-start | bytes 98312 | tf_op jit(solution)/shard_map/ppermute | solution.py:435
  65.9 0.6 copy-start.9
  66.5 0.7 copy-start.7
  (1 other events, 0.6 us)

commit v2 on v0

--- a/solution.py
+++ b/solution.py
@@ -104,8 +104,29 @@
     lax.fori_loop(0, depth, plane, 0)
 
 
-def pack(collided, sends, cell_refs):
-    send_x, send_up, send_down, corner_up, corner_down = sends
+def by_parity(place, even_case, odd_case):
+    for wanted, pairs in ((0, even_case), (1, odd_case)):
+
+        @pl.when(place[1] == wanted)
+        def _():
+            for target, source in pairs:
+                target[...] = source[...]
+
+
+def unpack(received, ordered, place):
+    recv_x, first, second, corner_first, corner_second = received
+    low, high, corner_low, corner_high = ordered
+    by_parity(
+        place,
+        ((high, first), (low, second), (corner_high, corner_first), (corner_low, corner_second)),
+        ((low, first), (high, second), (corner_low, corner_first), (corner_high, corner_second)),
+    )
+    return recv_x, low, high, corner_low, corner_high
+
+
+def pack(collided, sends, faces, place, cell_refs):
+    send_x, first_send, second_send, first_corner, second_corner = sends
+    send_up, send_down, corner_up, corner_down = faces
     depth, rows = collided.shape[1], collided.shape[2]
     for side, a, x in ((0, 1, depth - 1), (1, -1, 0)):
         for i in range(9):
@@ -129,9 +150,25 @@
                 corner[side, e + 1 : e + 2, :] = collided[k, x, y : y + 1, :]
             for i, ref in enumerate(cell_refs):
                 corner[side, 3 + i : 4 + i, :] = ref[x, y : y + 1, :].astype(jnp.float32)
-
-
-def first_kernel(populations, kind, profile, rates, collided, *sends):
+    by_parity(
+        place,
+        (
+            (first_send, send_up),
+            (second_send, send_down),
+            (first_corner, corner_up),
+            (second_corner, corner_down),
+        ),
+        (
+            (first_send, send_down),
+            (second_send, send_up),
+            (first_corner, corner_down),
+            (second_corner, corner_up),
+        ),
+    )
+
+
+def first_kernel(populations, kind, profile, rates, place, collided, *rest):
+    sends, faces = rest[:5], rest[5:]
     depth, cells = populations.shape[1], populations.shape[3]
 
     def body(x, span):
@@ -142,7 +179,7 @@
             collided[k, x, :, span] = values[k]
 
     tiles(depth, cells, body)
-    pack(collided, sends, (kind, profile))
+    pack(collided, sends, faces, place, (kind, profile))
 
 
 def shifted(plane, row, b, e, sublane):
@@ -283,31 +320,34 @@
 
 
 def second_kernel(*refs):
-    collided, *halo = refs[:6]
+    collided, *received = refs[:6]
     kind, profile, table, rates, place = refs[6:11]
     out, bounce = refs[11:13]
     sends = refs[13:18]
-    passed, kinds_row, profiles_row, planes, edges = refs[18:]
+    passed, kinds_row, profiles_row, planes, edges = refs[18:23]
+    halo = unpack(received, refs[23:27], place)
     make_fields(halo, kind, profile, table, place, kinds_row, profiles_row, planes, edges)
     stream(collided, halo, bounce, passed, (planes, edges))
     collide_cells(passed, kind, profile, table, rates, out)
-    pack(out, sends, ())
+    pack(out, sends, refs[27:], place, ())
 
 
 def middle_kernel(*refs):
-    collided, *halo = refs[:6]
-    bounce, kind, profile, table, rates = refs[6:11]
-    out = refs[11]
-    sends = refs[12:17]
-    passed = refs[17]
+    collided, *received = refs[:6]
+    bounce, kind, profile, table, rates, place = refs[6:12]
+    out = refs[12]
+    sends = refs[13:18]
+    passed = refs[18]
+    halo = unpack(received, refs[19:23], place)
     stream(collided, halo, bounce, passed, None)
     collide_cells(passed, kind, profile, table, rates, out)
-    pack(out, sends, ())
+    pack(out, sends, refs[23:], place, ())
 
 
 def last_kernel(*refs):
-    collided, *halo = refs[:6]
-    bounce, kind, profile, table, advanced, passed = refs[6:]
+    collided, *received = refs[:6]
+    bounce, kind, profile, table, place, advanced, passed = refs[6:13]
+    halo = unpack(received, refs[13:], place)
     stream(collided, halo, bounce, passed, None)
     finish_cells(passed, kind, profile, table, advanced)
 
@@ -318,22 +358,31 @@
     return lax.ppermute(value, "gx", pairs)
 
 
-def both_sides(value, across):
+def swapped(value, parity, across):
+    count = lax.axis_size("gx")
+    pairs = []
+    for source in range(parity, count, 2):
+        target = (source + 1) % count
+        if (target + PY // 2) % PY:
+            pairs.append((source, (target + across) % count))
+            pairs.append((target, (source + across) % count))
+    return lax.ppermute(value, "gx", pairs)
+
+
+def both_sides(value, send):
     if lax.axis_size("gx") == 2 * PY:
-        return passed_along(value, PY + across)
-    return jnp.stack(
-        [passed_along(value[0], PY + across), passed_along(value[1], across - PY)]
-    )
+        return send(value, PY)
+    return jnp.stack([send(value[0], PY), send(value[1], -PY)])
 
 
 def exchange(sends):
-    send_x, send_up, send_down, corner_up, corner_down = sends
+    send_x, first, second, corner_first, corner_second = sends
     return (
-        both_sides(send_x, 0),
-        passed_along(send_up, 1),
-        passed_along(send_down, -1),
-        both_sides(corner_up, 1),
-        both_sides(corner_down, -1),
+        both_sides(send_x, passed_along),
+        swapped(first, 0, 0),
+        swapped(second, 1, 0),
+        both_sides(corner_first, lambda value, across: swapped(value, 0, across)),
+        both_sides(corner_second, lambda value, across: swapped(value, 1, across)),
     )
 
 
@@ -349,13 +398,17 @@
     field = jax.ShapeDtypeStruct(scaled.shape, f32)
     vmem = pl.BlockSpec(memory_space=pltpu.VMEM)
     smem = pl.BlockSpec(memory_space=pltpu.SMEM)
-    place = ((lax.axis_index("gx") + PY // 2) % PY).astype(jnp.int32).reshape(1)
+    index = lax.axis_index("gx")
+    place = jnp.stack([(index + PY // 2) % PY, index % 2]).astype(jnp.int32)
 
     def send_shapes(extra):
         along = jax.ShapeDtypeStruct((round_up((9 + extra) * depth, 8), cells), f32)
         corner = jax.ShapeDtypeStruct((2, 8, cells), f32)
         across = jax.ShapeDtypeStruct((2, 9 + extra, rows, cells), f32)
         return (across, along, along, corner, corner)
+
+    def ordered(extra):
+        return [pltpu.VMEM(shape.shape, f32) for shape in send_shapes(extra)[1:]]
 
     def call(body, specs, outs, scratch, name):
         return pl.pallas_call(
@@ -370,8 +423,8 @@
     buffer = pltpu.VMEM(scaled.shape, f32)
     edge_rows = round_up(depth + 2, 8)
     collided, *sends = call(
-        first_kernel, [vmem] * 3 + [smem], (field,) + send_shapes(2), [], "first"
-    )(scaled, kind, profile, rates)
+        first_kernel, [vmem] * 3 + [smem] * 2, (field,) + send_shapes(2), ordered(2), "first"
+    )(scaled, kind, profile, rates, place)
     halo = exchange(sends)
     collided, bounce, *sends = call(
         second_kernel,
@@ -383,22 +436,24 @@
             pltpu.VMEM((edge_rows, cells), f32),
             pltpu.VMEM((4, depth + 2, rows, cells), f32),
             pltpu.VMEM((2, 4, edge_rows, cells), f32),
-        ],
+        ]
+        + ordered(2)
+        + ordered(0),
         "second",
     )(collided, *halo, kind, profile, vent_table, rates, place)
     for _ in range(STEPS - 2):
         halo = exchange(sends)
         collided, *sends = call(
             middle_kernel,
-            [vmem] * 9 + [smem] * 2,
+            [vmem] * 9 + [smem] * 3,
             (field,) + send_shapes(0),
-            [buffer],
+            [buffer] + ordered(0) * 2,
             "middle",
-        )(collided, *halo, bounce, kind, profile, vent_table, rates)
+        )(collided, *halo, bounce, kind, profile, vent_table, rates, place)
     halo = exchange(sends)
-    advanced = call(last_kernel, [vmem] * 9 + [smem], field, [buffer], "last")(
-        collided, *halo, bounce, kind, profile, vent_table
-    )
+    advanced = call(
+        last_kernel, [vmem] * 9 + [smem] * 2, field, [buffer] + ordered(0), "last"
+    )(collided, *halo, bounce, kind, profile, vent_table, place)
     return advanced[:, None]
 
 

time: 53.7 us -> 60 us (1.12)
  starting transfers between devices: 19.2 us -> 28.4 us
  waiting for transfers between devices: 17.7 us -> 14.4 us
  local copies, waits for them, and re-layouts: 3.35 us -> 2.66 us
    ppermute x0 -> x12, starting transfers between devices: none -> 21.7 us  [swapped(): return lax.ppermute(value, 'gx', pairs)]
    ppermute x15 -> x3, waiting for transfers between devices: 17.7 us -> 0.01 us  [passed_along(): return lax.ppermute(value, 'gx', pairs)]
    ppermute x0 -> x12, waiting for transfers between devices: none -> 14.4 us  [swapped(): return lax.ppermute(value, 'gx', pairs)]
    ppermute x15 -> x3, starting transfers between devices: 19.2 us -> 6.66 us  [passed_along(): return lax.ppermute(value, 'gx', pairs)]
    unnamed x33, local copies, waits for them, and re-layouts: 3.35 us -> 2.66 us
  transfers between devices with their start and end apart: 15 -> 15, of which waited for: 5 -> 6; matrix products, arithmetic and copies ran while one was open for 1% -> 1% of each run, Pallas kernels for 0% -> 0%
where the time goes in v2:
time: 60 us; the launch traced here: 59.6 us
  starting transfers between devices  28.4 us (47%)
  waiting for transfers between devices  14.4 us (24%)
  Pallas kernels  13.3 us (22%)
  local copies, waits for them, and re-layouts  2.66 us (4%)
    ppermute x12, starting transfers between devices, swapped(): return lax.ppermute(value, 'gx', pairs)  21.7 us
    ppermute x12, waiting for transfers between devices, swapped(): return lax.ppermute(value, 'gx', pairs)  14.4 us
    ppermute x3, starting transfers between devices, passed_along(): return lax.ppermute(value, 'gx', pairs)  6.66 us
    pallas_call x1, Pallas kernels, local(): call(second_kernel, [vmem] * 8 + [smem] * 3, (field, field) + send_shapes...  3.82 us
    pallas_call x1, Pallas kernels, local(): call(middle_kernel, [vmem] * 9 + [smem] * 3, (field,) + send_shapes(0), [...  3.56 us
    pallas_call x1, Pallas kernels, local(): call(last_kernel, [vmem] * 9 + [smem] * 2, field, [buffer] + ordered(0),...  3.19 us
    pallas_call x1, Pallas kernels, local(): call(first_kernel, [vmem] * 3 + [smem] * 2, (field,) + send_shapes(2), or...  2.75 us
    unnamed x33, local copies, waits for them, and re-layouts  2.66 us
  transfers between devices with their start and end apart: 15, of which 6 were waited for; matrix products, arithmetic and copies ran while one was open for 1% of the time, Pallas kernels for 0%

profile of v2, /device:TPU:1, one launch (start us, length us, event | category | flops | bytes accessed | tf_op | source)
XLA Modules:
  0.0 59.6 jit_solution(5766870623311824109)
XLA Ops:
  0.0 0.6 pad_add_fusion.place.refs_10_.refs_11_
  0.6 2.7 %first.1 = (f32[27,4,8,256]{3,2,1,0:T(8,128)}, f32[2,11,8,256]{3,2,1,0:T(8,128)}, f32[48,256]{1,0:T(8,128)}, f32[48,256]{1,0:T(8,128)}, f32[2,8,256]{2,1,0:T(8,128)}, /*index=5*/f32[2,8,256]{2,1,0:T(8,128)}) custom-call(f32[27,4,8,256]{3,2,1,0:T(8,128)} %bitcast.8, s32[4,8,256]{2,1,0:T(8,128)} %bitcast.9, s32[4,8,256]{2,1,0:T(8,128)} %bitcast.13, ...), custom_call_target="tpu_custom_call" | custom-call | tf_op jit(solution)/shard_map/first/pallas_call | solution.py:425
  3.3 3.1 %collective-permute-start = (f32[2,11,8,256]{3,2,1,0:T(8,128)}, f32[2,11,8,256]{3,2,1,0:T(8,128)S(1)}, u32[]{:S(2)}, u32[]{:S(2)}) collective-permute-start(f32[2,11,8,256]{3,2,1,0:T(8,128)} %get-tuple-element.25), channel_id=1, source_target_pairs={{0,8},{1,9},{2,10},{3,11},{4,12},{5,13},{6,14},{7,15},{8,0},{9,1},... | collective-permute-start | bytes 540680 | tf_op jit(solution)/shard_map/ppermute | solution.py:358
  6.5 1.0 %collective-permute-start.1 = (f32[48,256]{1,0:T(8,128)}, f32[48,256]{1,0:T(8,128)S(1)}, u32[]{:S(2)}, u32[]{:S(2)}) collective-permute-start(f32[48,256]{1,0:T(8,128)} %get-tuple-element.26), channel_id=1, source_target_pairs={{0,1},{1,0},{2,3},{3,2},{4,5},{5,4},{6,7},{7,6},{8,9},{9,8},{10,11... | collective-permute-start | bytes 147464 | tf_op jit(solution)/shard_map/ppermute | solution.py:369
  7.4 3.2 %collective-permute-start.2 = (f32[48,256]{1,0:T(8,128)}, f32[48,256]{1,0:T(8,128)S(1)}, u32[]{:S(2)}, u32[]{:S(2)}) collective-permute-start(f32[48,256]{1,0:T(8,128)} %get-tuple-element.27), channel_id=1, source_target_pairs={{1,2},{2,1},{5,6},{6,5},{7,8},{8,7},{9,10},{10,9},{13,14},{14,13},... | collective-permute-start | bytes 147464 | tf_op jit(solution)/shard_map/ppermute | solution.py:369
  10.6 2.7 %collective-permute-start.3 = (f32[2,8,256]{2,1,0:T(8,128)}, f32[2,8,256]{2,1,0:T(8,128)S(1)}, u32[]{:S(2)}, u32[]{:S(2)}) collective-permute-start(f32[2,8,256]{2,1,0:T(8,128)} %get-tuple-element.28), channel_id=1, source_target_pairs={{0,9},{1,8},{2,11},{3,10},{4,13},{5,12},{6,15},{7,14},{8,1},{9,0},... | collective-permute-start | bytes 49160 | tf_op jit(solution)/shard_map/ppermute | solution.py:369
  13.2 1.9 %collective-permute-start.4 = (f32[2,8,256]{2,1,0:T(8,128)}, f32[2,8,256]{2,1,0:T(8,128)S(1)}, u32[]{:S(2)}, u32[]{:S(2)}) collective-permute-start(f32[2,8,256]{2,1,0:T(8,128)} %get-tuple-element.29), channel_id=1, source_target_pairs={{1,10},{2,9},{5,14},{6,13},{7,0},{8,15},{9,2},{10,1},{13,6},{14,5}... | collective-permute-start | bytes 49160 | tf_op jit(solution)/shard_map/ppermute | solution.py:369
  15.2 0.7 %copy.6.refs_8_.refs_9_ = f32[8,3]{1,0:T(8,128)} copy(f32[8,3]{0,1:T(4,128)S(1)} %copy-done.15) | data formatting | bytes 192 | tf_op args[3]
  15.8 0.7 %collective-permute-done.3.refs_4_ = f32[2,8,256]{2,1,0:T(8,128)S(1)} collective-permute-done((f32[2,8,256]{2,1,0:T(8,128)}, f32[2,8,256]{2,1,0:T(8,128)S(1)}, u32[]{:S(2)}, u32[]{:S(2)}) %collective-permute-start.3) | collective-permute-done | bytes 16416 | tf_op jit(solution)/shard_map/ppermute | solution.py:369
  16.6 3.7 %collective-permute-done.4.refs_5_ = f32[2,8,256]{2,1,0:T(8,128)S(1)} collective-permute-done((f32[2,8,256]{2,1,0:T(8,128)}, f32[2,8,256]{2,1,0:T(8,128)S(1)}, u32[]{:S(2)}, u32[]{:S(2)}) %collective-permute-start.4) | collective-permute-done | bytes 16416 | tf_op jit(solution)/shard_map/ppermute | solution.py:369
  21.0 3.8 %second.1 = (f32[27,4,8,256]{3,2,1,0:T(8,128)}, f32[27,4,8,256]{3,2,1,0:T(8,128)}, f32[2,9,8,256]{3,2,1,0:T(8,128)}, f32[40,256]{1,0:T(8,128)}, f32[40,256]{1,0:...) custom-call(f32[27,4,8,256]{3,2,1,0:T(8,128)} %get-tuple-element.24.refs_0_, f32[2,11,8,256]{3,2,1,0:T(8,128)} %copy-done, ...), custom_call_target="tpu_custom_call" | custom-call | tf_op jit(solution)/shard_map/second/pallas_call | solution.py:429
  24.8 1.0 %collective-permute-start.5 = (f32[2,9,8,256]{3,2,1,0:T(8,128)}, f32[2,9,8,256]{3,2,1,0:T(8,128)S(1)}, u32[]{:S(2)}, u32[]{:S(2)}) collective-permute-start(f32[2,9,8,256]{3,2,1,0:T(8,128)} %get-tuple-element.31), channel_id=1, source_target_pairs={{0,8},{1,9},{2,10},{3,11},{4,12},{5,13},{6,14},{7,15},{8,0},{9,1},... | collective-permute-start | bytes 442376 | tf_op jit(solution)/shard_map/ppermute | solution.py:358
  25.8 1.9 %collective-permute-start.7 = (f32[40,256]{1,0:T(8,128)}, f32[40,256]{1,0:T(8,128)S(1)}, u32[]{:S(2)}, u32[]{:S(2)}) collective-permute-start(f32[40,256]{1,0:T(8,128)} %get-tuple-element.33), channel_id=1, source_target_pairs={{1,2},{2,1},{5,6},{6,5},{7,8},{8,7},{9,10},{10,9},{13,14},{14,13},... | collective-permute-start | bytes 122888 | tf_op jit(solution)/shard_map/ppermute | solution.py:369
  27.7 2.6 %collective-permute-start.8 = (f32[2,8,256]{2,1,0:T(8,128)}, f32[2,8,256]{2,1,0:T(8,128)S(1)}, u32[]{:S(2)}, u32[]{:S(2)}) collective-permute-start(f32[2,8,256]{2,1,0:T(8,128)} %get-tuple-element.34), channel_id=1, source_target_pairs={{0,9},{1,8},{2,11},{3,10},{4,13},{5,12},{6,15},{7,14},{8,1},{9,0},... | collective-permute-start | bytes 49160 | tf_op jit(solution)/shard_map/ppermute | solution.py:369
  30.4 2.2 %collective-permute-start.9 = (f32[2,8,256]{2,1,0:T(8,128)}, f32[2,8,256]{2,1,0:T(8,128)S(1)}, u32[]{:S(2)}, u32[]{:S(2)}) collective-permute-start(f32[2,8,256]{2,1,0:T(8,128)} %get-tuple-element.35), channel_id=1, source_target_pairs={{1,10},{2,9},{5,14},{6,13},{7,0},{8,15},{9,2},{10,1},{13,6},{14,5}... | collective-permute-start | bytes 49160 | tf_op jit(solution)/shard_map/ppermute | solution.py:369
  32.6 1.5 %collective-permute-done.8.refs_4_ = f32[2,8,256]{2,1,0:T(8,128)S(1)} collective-permute-done((f32[2,8,256]{2,1,0:T(8,128)}, f32[2,8,256]{2,1,0:T(8,128)S(1)}, u32[]{:S(2)}, u32[]{:S(2)}) %collective-permute-start.8) | collective-permute-done | bytes 16416 | tf_op jit(solution)/shard_map/ppermute | solution.py:369
  34.1 3.3 %collective-permute-done.9.refs_5_ = f32[2,8,256]{2,1,0:T(8,128)S(1)} collective-permute-done((f32[2,8,256]{2,1,0:T(8,128)}, f32[2,8,256]{2,1,0:T(8,128)S(1)}, u32[]{:S(2)}, u32[]{:S(2)}) %collective-permute-start.9) | collective-permute-done | bytes 16416 | tf_op jit(solution)/shard_map/ppermute | solution.py:369
  38.1 3.6 %middle.1 = (f32[27,4,8,256]{3,2,1,0:T(8,128)}, f32[2,9,8,256]{3,2,1,0:T(8,128)}, f32[40,256]{1,0:T(8,128)}, f32[40,256]{1,0:T(8,128)}, f32[2,8,256]{2,1,0:T(8,128)}, /*index=5*/f32[2,8,256]{2,1,0:T(8,128)}) custom-call(f32[27,4,8,256]{3,2,1,0:T(8,128)} %get-tuple-element.30.refs_0_, f32[2,9,8,256]{3,2,1,0:T(8,128)} %copy-done.2, f32[40,256]{1,0:T(8,128)} %copy-done.7, ...), custom_call_target="tpu_custom_call" | custom-call | tf_op jit(solution)/shard_map/middle/pallas_call | solution.py:446
  41.7 2.5 %collective-permute-start.10 = (f32[2,9,8,256]{3,2,1,0:T(8,128)}, f32[2,9,8,256]{3,2,1,0:T(8,128)S(1)}, u32[]{:S(2)}, u32[]{:S(2)}) collective-permute-start(f32[2,9,8,256]{3,2,1,0:T(8,128)} %get-tuple-element.38), channel_id=1, source_target_pairs={{0,8},{1,9},{2,10},{3,11},{4,12},{5,13},{6,14},{7,15},{8,0},{9,1},... | collective-permute-start | bytes 442376 | tf_op jit(solution)/shard_map/ppermute | solution.py:358
  44.2 1.9 %collective-permute-start.12 = (f32[40,256]{1,0:T(8,128)}, f32[40,256]{1,0:T(8,128)S(1)}, u32[]{:S(2)}, u32[]{:S(2)}) collective-permute-start(f32[40,256]{1,0:T(8,128)} %get-tuple-element.40), channel_id=1, source_target_pairs={{1,2},{2,1},{5,6},{6,5},{7,8},{8,7},{9,10},{10,9},{13,14},{14,13},... | collective-permute-start | bytes 122888 | tf_op jit(solution)/shard_map/ppermute | solution.py:369
  46.1 2.5 %collective-permute-start.13 = (f32[2,8,256]{2,1,0:T(8,128)}, f32[2,8,256]{2,1,0:T(8,128)S(1)}, u32[]{:S(2)}, u32[]{:S(2)}) collective-permute-start(f32[2,8,256]{2,1,0:T(8,128)} %get-tuple-element.41), channel_id=1, source_target_pairs={{0,9},{1,8},{2,11},{3,10},{4,13},{5,12},{6,15},{7,14},{8,1},{9,0},... | collective-permute-start | bytes 49160 | tf_op jit(solution)/shard_map/ppermute | solution.py:369
  48.6 1.9 %collective-permute-start.14 = (f32[2,8,256]{2,1,0:T(8,128)}, f32[2,8,256]{2,1,0:T(8,128)S(1)}, u32[]{:S(2)}, u32[]{:S(2)}) collective-permute-start(f32[2,8,256]{2,1,0:T(8,128)} %get-tuple-element.42), channel_id=1, source_target_pairs={{1,10},{2,9},{5,14},{6,13},{7,0},{8,15},{9,2},{10,1},{13,6},{14,5}... | collective-permute-start | bytes 49160 | tf_op jit(solution)/shard_map/ppermute | solution.py:369
  50.8 4.9 %collective-permute-done.14.refs_5_ = f32[2,8,256]{2,1,0:T(8,128)S(1)} collective-permute-done((f32[2,8,256]{2,1,0:T(8,128)}, f32[2,8,256]{2,1,0:T(8,128)S(1)}, u32[]{:S(2)}, u32[]{:S(2)}) %collective-permute-start.14) | collective-permute-done | bytes 16416 | tf_op jit(solution)/shard_map/ppermute | solution.py:369
  56.4 3.2 %last.1 = f32[27,4,8,256]{3,2,1,0:T(8,128)} custom-call(f32[27,4,8,256]{3,2,1,0:T(8,128)} %get-tuple-element.37.refs_0_, f32[2,9,8,256]{3,2,1,0:T(8,128)} %copy-done.1, f32[40,256]{1,0:T(8,128)} %copy-done.5, f32[40,256]{1,0:T(8,128)} %copy-done.6, f32[2,8,256]{2,1,0:T(8,128)} %copy-done.13, f32[2,8,256]{2,1,0:T(8,128)} %copy-done.14, ...), custom_call_target="tpu_custom_call" | custom-call | tf_op jit(solution)/shard_map/last/pallas_call | solution.py:454
  (44 shorter events, 2.3 us)
Async XLA Ops:
  3.3 17.0 %collective-permute-start = (f32[2,11,8,256]{3,2,1,0:T(8,128)}, f32[2,11,8,256]{3,2,1,0:T(8,128)S(1)}, u32[]{:S(2)}, u32[]{:S(2)}) collective-permute-start(f32[2,11,8,256]{3,2,1,0:T(8,128)} %get-tuple-element.25), channel_id=1, source_target_pairs={{0,8},{1,9},{2,10},{3,11},{4,12},{5,13},{6,14},{7,15},{8,0},{9,1},... | collective-permute-start | bytes 540680 | tf_op jit(solution)/shard_map/ppermute | solution.py:358
  6.5 13.8 %collective-permute-start.1 = (f32[48,256]{1,0:T(8,128)}, f32[48,256]{1,0:T(8,128)S(1)}, u32[]{:S(2)}, u32[]{:S(2)}) collective-permute-start(f32[48,256]{1,0:T(8,128)} %get-tuple-element.26), channel_id=1, source_target_pairs={{0,1},{1,0},{2,3},{3,2},{4,5},{5,4},{6,7},{7,6},{8,9},{9,8},{10,11... | collective-permute-start | bytes 147464 | tf_op jit(solution)/shard_map/ppermute | solution.py:369
  7.4 7.7 %copy-start.15 = (f32[8,3]{0,1:T(4,128)S(1)}, f32[8,3]{0,1:T(4,128)}, u32[]{:S(2)}) copy-start(f32[8,3]{0,1:T(4,128)} %param.8) | copy-start | bytes 292
  7.4 12.9 %collective-permute-start.2 = (f32[48,256]{1,0:T(8,128)}, f32[48,256]{1,0:T(8,128)S(1)}, u32[]{:S(2)}, u32[]{:S(2)}) collective-permute-start(f32[48,256]{1,0:T(8,128)} %get-tuple-element.27), channel_id=1, source_target_pairs={{1,2},{2,1},{5,6},{6,5},{7,8},{8,7},{9,10},{10,9},{13,14},{14,13},... | collective-permute-start | bytes 147464 | tf_op jit(solution)/shard_map/ppermute | solution.py:369
  10.6 6.0 %collective-permute-start.3 = (f32[2,8,256]{2,1,0:T(8,128)}, f32[2,8,256]{2,1,0:T(8,128)S(1)}, u32[]{:S(2)}, u32[]{:S(2)}) collective-permute-start(f32[2,8,256]{2,1,0:T(8,128)} %get-tuple-element.28), channel_id=1, source_target_pairs={{0,9},{1,8},{2,11},{3,10},{4,13},{5,12},{6,15},{7,14},{8,1},{9,0},... | collective-permute-start | bytes 49160 | tf_op jit(solution)/shard_map/ppermute | solution.py:369
  13.2 7.1 %collective-permute-start.4 = (f32[2,8,256]{2,1,0:T(8,128)}, f32[2,8,256]{2,1,0:T(8,128)S(1)}, u32[]{:S(2)}, u32[]{:S(2)}) collective-permute-start(f32[2,8,256]{2,1,0:T(8,128)} %get-tuple-element.29), channel_id=1, source_target_pairs={{1,10},{2,9},{5,14},{6,13},{7,0},{8,15},{9,2},{10,1},{13,6},{14,5}... | collective-permute-start | bytes 49160 | tf_op jit(solution)/shard_map/ppermute | solution.py:369
  16.6 3.8 %copy-start.9 = (f32[2,8,256]{2,1,0:T(8,128)}, f32[2,8,256]{2,1,0:T(8,128)S(1)}, u32[]{:S(2)}) copy-start(f32[2,8,256]{2,1,0:T(8,128)S(1)} %collective-permute-done.3.refs_4_) | copy-start | bytes 49156
  20.3 0.6 %copy-start.3 = (f32[48,256]{1,0:T(8,128)}, f32[48,256]{1,0:T(8,128)S(1)}, u32[]{:S(2)}) copy-start(f32[48,256]{1,0:T(8,128)S(1)} %collective-permute-done.1.refs_2_) | copy-start | bytes 147460
  20.3 0.6 %copy-start.4 = (f32[48,256]{1,0:T(8,128)}, f32[48,256]{1,0:T(8,128)S(1)}, u32[]{:S(2)}) copy-start(f32[48,256]{1,0:T(8,128)S(1)} %collective-permute-done.2.refs_3_) | copy-start | bytes 147460
  20.3 0.7 %copy-start = (f32[2,11,8,256]{3,2,1,0:T(8,128)}, f32[2,11,8,256]{3,2,1,0:T(8,128)S(1)}, u32[]{:S(2)}) copy-start(f32[2,11,8,256]{3,2,1,0:T(8,128)S(1)} %collective-permute-done.refs_1_) | copy-start | bytes 540676
  24.8 12.6 %collective-permute-start.5 = (f32[2,9,8,256]{3,2,1,0:T(8,128)}, f32[2,9,8,256]{3,2,1,0:T(8,128)S(1)}, u32[]{:S(2)}, u32[]{:S(2)}) collective-permute-start(f32[2,9,8,256]{3,2,1,0:T(8,128)} %get-tuple-element.31), channel_id=1, source_target_pairs={{0,8},{1,9},{2,10},{3,11},{4,12},{5,13},{6,14},{7,15},{8,0},{9,1},... | collective-permute-start | bytes 442376 | tf_op jit(solution)/shard_map/ppermute | solution.py:358
  25.8 11.6 %collective-permute-start.6 = (f32[40,256]{1,0:T(8,128)}, f32[40,256]{1,0:T(8,128)S(1)}, u32[]{:S(2)}, u32[]{:S(2)}) collective-permute-start(f32[40,256]{1,0:T(8,128)} %get-tuple-element.32), channel_id=1, source_target_pairs={{0,1},{1,0},{2,3},{3,2},{4,5},{5,4},{6,7},{7,6},{8,9},{9,8},{10,11... | collective-permute-start | bytes 122888 | tf_op jit(solution)/shard_map/ppermute | solution.py:369
  25.8 11.6 %collective-permute-start.7 = (f32[40,256]{1,0:T(8,128)}, f32[40,256]{1,0:T(8,128)S(1)}, u32[]{:S(2)}, u32[]{:S(2)}) collective-permute-start(f32[40,256]{1,0:T(8,128)} %get-tuple-element.33), channel_id=1, source_target_pairs={{1,2},{2,1},{5,6},{6,5},{7,8},{8,7},{9,10},{10,9},{13,14},{14,13},... | collective-permute-start | bytes 122888 | tf_op jit(solution)/shard_map/ppermute | solution.py:369
  27.7 6.4 %collective-permute-start.8 = (f32[2,8,256]{2,1,0:T(8,128)}, f32[2,8,256]{2,1,0:T(8,128)S(1)}, u32[]{:S(2)}, u32[]{:S(2)}) collective-permute-start(f32[2,8,256]{2,1,0:T(8,128)} %get-tuple-element.34), channel_id=1, source_target_pairs={{0,9},{1,8},{2,11},{3,10},{4,13},{5,12},{6,15},{7,14},{8,1},{9,0},... | collective-permute-start | bytes 49160 | tf_op jit(solution)/shard_map/ppermute | solution.py:369
  30.4 7.1 %collective-permute-start.9 = (f32[2,8,256]{2,1,0:T(8,128)}, f32[2,8,256]{2,1,0:T(8,128)S(1)}, u32[]{:S(2)}, u32[]{:S(2)}) collective-permute-start(f32[2,8,256]{2,1,0:T(8,128)} %get-tuple-element.35), channel_id=1, source_target_pairs={{1,10},{2,9},{5,14},{6,13},{7,0},{8,15},{9,2},{10,1},{13,6},{14,5}... | collective-permute-start | bytes 49160 | tf_op jit(solution)/shard_map/ppermute | solution.py:369
  34.1 3.3 %copy-start.10 = (f32[2,8,256]{2,1,0:T(8,128)}, f32[2,8,256]{2,1,0:T(8,128)S(1)}, u32[]{:S(2)}) copy-start(f32[2,8,256]{2,1,0:T(8,128)S(1)} %collective-permute-done.8.refs_4_) | copy-start | bytes 49156
  37.4 0.7 %copy-start.2 = (f32[2,9,8,256]{3,2,1,0:T(8,128)}, f32[2,9,8,256]{3,2,1,0:T(8,128)S(1)}, u32[]{:S(2)}) copy-start(f32[2,9,8,256]{3,2,1,0:T(8,128)S(1)} %collective-permute-done.5.refs_1_) | copy-start | bytes 442372
  41.7 14.0 %collective-permute-start.10 = (f32[2,9,8,256]{3,2,1,0:T(8,128)}, f32[2,9,8,256]{3,2,1,0:T(8,128)S(1)}, u32[]{:S(2)}, u32[]{:S(2)}) collective-permute-start(f32[2,9,8,256]{3,2,1,0:T(8,128)} %get-tuple-element.38), channel_id=1, source_target_pairs={{0,8},{1,9},{2,10},{3,11},{4,12},{5,13},{6,14},{7,15},{8,0},{9,1},... | collective-permute-start | bytes 442376 | tf_op jit(solution)/shard_map/ppermute | solution.py:358
  44.2 11.5 %collective-permute-start.11 = (f32[40,256]{1,0:T(8,128)}, f32[40,256]{1,0:T(8,128)S(1)}, u32[]{:S(2)}, u32[]{:S(2)}) collective-permute-start(f32[40,256]{1,0:T(8,128)} %get-tuple-element.39), channel_id=1, source_target_pairs={{0,1},{1,0},{2,3},{3,2},{4,5},{5,4},{6,7},{7,6},{8,9},{9,8},{10,11... | collective-permute-start | bytes 122888 | tf_op jit(solution)/shard_map/ppermute | solution.py:369
  44.2 11.5 %collective-permute-start.12 = (f32[40,256]{1,0:T(8,128)}, f32[40,256]{1,0:T(8,128)S(1)}, u32[]{:S(2)}, u32[]{:S(2)}) collective-permute-start(f32[40,256]{1,0:T(8,128)} %get-tuple-element.40), channel_id=1, source_target_pairs={{1,2},{2,1},{5,6},{6,5},{7,8},{8,7},{9,10},{10,9},{13,14},{14,13},... | collective-permute-start | bytes 122888 | tf_op jit(solution)/shard_map/ppermute | solution.py:369
  46.1 4.6 %collective-permute-start.13 = (f32[2,8,256]{2,1,0:T(8,128)}, f32[2,8,256]{2,1,0:T(8,128)S(1)}, u32[]{:S(2)}, u32[]{:S(2)}) collective-permute-start(f32[2,8,256]{2,1,0:T(8,128)} %get-tuple-element.41), channel_id=1, source_target_pairs={{0,9},{1,8},{2,11},{3,10},{4,13},{5,12},{6,15},{7,14},{8,1},{9,0},... | collective-permute-start | bytes 49160 | tf_op jit(solution)/shard_map/ppermute | solution.py:369
  48.6 7.1 %collective-permute-start.14 = (f32[2,8,256]{2,1,0:T(8,128)}, f32[2,8,256]{2,1,0:T(8,128)S(1)}, u32[]{:S(2)}, u32[]{:S(2)}) collective-permute-start(f32[2,8,256]{2,1,0:T(8,128)} %get-tuple-element.42), channel_id=1, source_target_pairs={{1,10},{2,9},{5,14},{6,13},{7,0},{8,15},{9,2},{10,1},{13,6},{14,5}... | collective-permute-start | bytes 49160 | tf_op jit(solution)/shard_map/ppermute | solution.py:369
  50.8 4.9 %copy-start.13 = (f32[2,8,256]{2,1,0:T(8,128)}, f32[2,8,256]{2,1,0:T(8,128)S(1)}, u32[]{:S(2)}) copy-start(f32[2,8,256]{2,1,0:T(8,128)S(1)} %collective-permute-done.13.refs_4_) | copy-start | bytes 49156
  55.7 0.7 %copy-start.1 = (f32[2,9,8,256]{3,2,1,0:T(8,128)}, f32[2,9,8,256]{3,2,1,0:T(8,128)S(1)}, u32[]{:S(2)}) copy-start(f32[2,9,8,256]{3,2,1,0:T(8,128)S(1)} %collective-permute-done.10.refs_1_) | copy-start | bytes 442372
  (7 other events, 4.3 us)

commit v3 on v0

--- a/solution.py
+++ b/solution.py
@@ -326,15 +326,20 @@
     )
 
 
+def resident(value):
+    return pltpu.with_memory_space_constraint(value, pltpu.VMEM)
+
+
 def exchange(sends):
     send_x, send_up, send_down, corner_up, corner_down = sends
-    return (
+    received = (
         both_sides(send_x, 0),
         passed_along(send_up, 1),
         passed_along(send_down, -1),
         both_sides(corner_up, 1),
         both_sides(corner_down, -1),
     )
+    return tuple(pltpu.with_memory_space_constraint(h, pltpu.VMEM) for h in received)
 
 
 def round_up(value, step):
@@ -372,6 +377,7 @@
     collided, *sends = call(
         first_kernel, [vmem] * 3 + [smem], (field,) + send_shapes(2), [], "first"
     )(scaled, kind, profile, rates)
+    collided = resident(collided)
     halo = exchange(sends)
     collided, bounce, *sends = call(
         second_kernel,
@@ -386,7 +392,9 @@
         ],
         "second",
     )(collided, *halo, kind, profile, vent_table, rates, place)
+    bounce = resident(bounce)
     for _ in range(STEPS - 2):
+        collided = resident(collided)
         halo = exchange(sends)
         collided, *sends = call(
             middle_kernel,
@@ -395,6 +403,7 @@
             [buffer],
             "middle",
         )(collided, *halo, bounce, kind, profile, vent_table, rates)
+    collided = resident(collided)
     halo = exchange(sends)
     advanced = call(last_kernel, [vmem] * 9 + [smem], field, [buffer], "last")(
         collided, *halo, bounce, kind, profile, vent_table

time: 53.7 us -> 54.3 us (1.011)
  local copies, waits for them, and re-layouts: 3.35 us -> 6.01 us
  Pallas kernels: 13 us -> 10.9 us
    unnamed x33 -> x13, local copies, waits for them, and re-layouts: 3.35 us -> 6.01 us
    pallas_call x1, Pallas kernels: 3.48 us -> 2.66 us  [local(): call(middle_kernel, [vmem] * 9 + [smem] * 2, (field,) + send_shapes(0), [...]
    pallas_call x1, Pallas kernels: 3.16 us -> 2.4 us  [local(): call(last_kernel, [vmem] * 9 + [smem], field, [buffer], 'last')]
where the time goes in v3:
time: 54.3 us; the launch traced here: 53.8 us
  starting transfers between devices  19.2 us (35%)
  waiting for transfers between devices  17.7 us (33%)
  Pallas kernels  10.9 us (20%)
  local copies, waits for them, and re-layouts  6.01 us (11%)
    ppermute x15, starting transfers between devices, passed_along(): return lax.ppermute(value, 'gx', pairs)  19.2 us
    ppermute x15, waiting for transfers between devices, passed_along(): return lax.ppermute(value, 'gx', pairs)  17.7 us
    unnamed x13, local copies, waits for them, and re-layouts  6.01 us
    pallas_call x1, Pallas kernels, local(): call(second_kernel, [vmem] * 8 + [smem] * 3, (field, field) + send_shapes...  3.17 us
    pallas_call x1, Pallas kernels, local(): call(first_kernel, [vmem] * 3 + [smem], (field,) + send_shapes(2), [], 'f...  2.66 us
    pallas_call x1, Pallas kernels, local(): call(middle_kernel, [vmem] * 9 + [smem] * 2, (field,) + send_shapes(0), [...  2.66 us
    pallas_call x1, Pallas kernels, local(): call(last_kernel, [vmem] * 9 + [smem], field, [buffer], 'last')  2.4 us
  transfers between devices with their start and end apart: 15, of which 5 were waited for; matrix products, arithmetic and copies ran while one was open for 1% of the time, Pallas kernels for 0%

profile of v3, /device:TPU:1, one launch (start us, length us, event | category | flops | bytes accessed | tf_op | source)
XLA Modules:
  0.0 53.8 jit_solution(10234272717965769494)
XLA Ops:
  0.0 2.7 %first.1 = (f32[27,4,8,256]{3,2,1,0:T(8,128)}, f32[2,11,8,256]{3,2,1,0:T(8,128)}, f32[48,256]{1,0:T(8,128)}, f32[48,256]{1,0:T(8,128)}, f32[2,8,256]{2,1,0:T(8,128)}, /*index=5*/f32[2,8,256]{2,1,0:T(8,128)}) custom-call(f32[27,4,8,256]{3,2,1,0:T(8,128)} %bitcast.7, s32[4,8,256]{2,1,0:T(8,128)} %bitcast.8, s32[4,8,256]{2,1,0:T(8,128)} %bitcast.12, f32[27]{0:T(128)} %refs_10_.1), custom_call_target="tpu_custom_call" | custom-call | tf_op jit(solution)/shard_map/first/pallas_call | solution.py:377
  2.7 3.1 %collective-permute-start = (f32[2,11,8,256]{3,2,1,0:T(8,128)}, f32[2,11,8,256]{3,2,1,0:T(8,128)S(1)}, u32[]{:S(2)}, u32[]{:S(2)}) collective-permute-start(f32[2,11,8,256]{3,2,1,0:T(8,128)} %get-tuple-element.25), channel_id=1, source_target_pairs={{0,8},{1,9},{2,10},{3,11},{4,12},{5,13},{6,14},{7,15},{8,0},{9,1},... | collective-permute-start | bytes 540680 | tf_op jit(solution)/shard_map/ppermute | solution.py:318
  5.8 2.1 %collective-permute-start.1 = (f32[48,256]{1,0:T(8,128)}, f32[48,256]{1,0:T(8,128)S(1)}, u32[]{:S(2)}, u32[]{:S(2)}) collective-permute-start(f32[48,256]{1,0:T(8,128)} %get-tuple-element.26), channel_id=1, source_target_pairs={{0,1},{1,2},{2,3},{3,4},{4,5},{5,6},{6,7},{7,8},{8,9},{9,10},{10,1... | collective-permute-start | bytes 147464 | tf_op jit(solution)/shard_map/ppermute | solution.py:318
  7.9 1.5 %collective-permute-start.3 = (f32[2,8,256]{2,1,0:T(8,128)}, f32[2,8,256]{2,1,0:T(8,128)S(1)}, u32[]{:S(2)}, u32[]{:S(2)}) collective-permute-start(f32[2,8,256]{2,1,0:T(8,128)} %get-tuple-element.28), channel_id=1, source_target_pairs={{0,9},{1,10},{2,11},{3,12},{4,13},{5,14},{6,15},{7,0},{8,1},{9,2},... | collective-permute-start | bytes 49160 | tf_op jit(solution)/shard_map/ppermute | solution.py:318
  9.4 1.1 %collective-permute-start.4 = (f32[2,8,256]{2,1,0:T(8,128)}, f32[2,8,256]{2,1,0:T(8,128)S(1)}, u32[]{:S(2)}, u32[]{:S(2)}) collective-permute-start(f32[2,8,256]{2,1,0:T(8,128)} %get-tuple-element.29), channel_id=1, source_target_pairs={{0,7},{1,8},{2,9},{3,10},{4,11},{5,12},{6,13},{7,14},{8,15},{9,0},... | collective-permute-start | bytes 49160 | tf_op jit(solution)/shard_map/ppermute | solution.py:318
  10.5 0.7 %copy-done.5 = f32[8,3]{0,1:T(4,128)S(1)} copy-done((f32[8,3]{0,1:T(4,128)S(1)}, f32[8,3]{0,1:T(4,128)}, u32[]{:S(2)}) %copy-start.5) | copy-done | bytes 120
  11.2 0.7 %copy.6.refs_8_.refs_9_ = f32[8,3]{1,0:T(8,128)} copy(f32[8,3]{0,1:T(4,128)S(1)} %copy-done.5) | data formatting | bytes 192 | tf_op args[3]
  11.9 4.4 %collective-permute-done.3.refs_4_ = f32[2,8,256]{2,1,0:T(8,128)S(1)} collective-permute-done((f32[2,8,256]{2,1,0:T(8,128)}, f32[2,8,256]{2,1,0:T(8,128)S(1)}, u32[]{:S(2)}, u32[]{:S(2)}) %collective-permute-start.3) | collective-permute-done | bytes 16416 | tf_op jit(solution)/shard_map/ppermute | solution.py:318
  16.3 1.2 %collective-permute-done.4.refs_5_ = f32[2,8,256]{2,1,0:T(8,128)S(1)} collective-permute-done((f32[2,8,256]{2,1,0:T(8,128)}, f32[2,8,256]{2,1,0:T(8,128)S(1)}, u32[]{:S(2)}, u32[]{:S(2)}) %collective-permute-start.4) | collective-permute-done | bytes 16416 | tf_op jit(solution)/shard_map/ppermute | solution.py:318
  17.5 1.2 %copy-done.4 = f32[27,4,8,256]{3,2,1,0:T(8,128)S(1)} copy-done((f32[27,4,8,256]{3,2,1,0:T(8,128)S(1)}, f32[27,4,8,256]{3,2,1,0:T(8,128)}, u32[]{:S(2)}) %copy-start.4) | copy-done | bytes 884760
  18.6 3.2 %second.1 = (f32[27,4,8,256]{3,2,1,0:T(8,128)}, f32[27,4,8,256]{3,2,1,0:T(8,128)}, f32[2,9,8,256]{3,2,1,0:T(8,128)}, f32[40,256]{1,0:T(8,128)}, f32[40,256]{1,0:...) custom-call(f32[27,4,8,256]{3,2,1,0:T(8,128)S(1)} %copy-done.4, ...), custom_call_target="tpu_custom_call" | custom-call | tf_op jit(solution)/shard_map/second/pallas_call | solution.py:382
  22.3 2.6 %collective-permute-start.7 = (f32[40,256]{1,0:T(8,128)}, f32[40,256]{1,0:T(8,128)S(1)}, u32[]{:S(2)}, u32[]{:S(2)}) collective-permute-start(f32[40,256]{1,0:T(8,128)} %get-tuple-element.33), channel_id=1, source_target_pairs={{0,15},{1,0},{2,1},{3,2},{4,3},{5,4},{6,5},{7,6},{8,7},{9,8},{10,9... | collective-permute-start | bytes 122888 | tf_op jit(solution)/shard_map/ppermute | solution.py:318
  24.9 1.5 %collective-permute-start.8 = (f32[2,8,256]{2,1,0:T(8,128)}, f32[2,8,256]{2,1,0:T(8,128)S(1)}, u32[]{:S(2)}, u32[]{:S(2)}) collective-permute-start(f32[2,8,256]{2,1,0:T(8,128)} %get-tuple-element.34), channel_id=1, source_target_pairs={{0,9},{1,10},{2,11},{3,12},{4,13},{5,14},{6,15},{7,0},{8,1},{9,2},... | collective-permute-start | bytes 49160 | tf_op jit(solution)/shard_map/ppermute | solution.py:318
  26.4 1.1 %collective-permute-start.9 = (f32[2,8,256]{2,1,0:T(8,128)}, f32[2,8,256]{2,1,0:T(8,128)S(1)}, u32[]{:S(2)}, u32[]{:S(2)}) collective-permute-start(f32[2,8,256]{2,1,0:T(8,128)} %get-tuple-element.35), channel_id=1, source_target_pairs={{0,7},{1,8},{2,9},{3,10},{4,11},{5,12},{6,13},{7,14},{8,15},{9,0},... | collective-permute-start | bytes 49160 | tf_op jit(solution)/shard_map/ppermute | solution.py:318
  27.5 5.9 %collective-permute-done.8.refs_4_ = f32[2,8,256]{2,1,0:T(8,128)S(1)} collective-permute-done((f32[2,8,256]{2,1,0:T(8,128)}, f32[2,8,256]{2,1,0:T(8,128)S(1)}, u32[]{:S(2)}, u32[]{:S(2)}) %collective-permute-start.8) | collective-permute-done | bytes 16416 | tf_op jit(solution)/shard_map/ppermute | solution.py:318
  33.4 1.2 %copy-done = f32[27,4,8,256]{3,2,1,0:T(8,128)S(1)} copy-done((f32[27,4,8,256]{3,2,1,0:T(8,128)S(1)}, f32[27,4,8,256]{3,2,1,0:T(8,128)}, u32[]{:S(2)}) %copy-start) | copy-done | bytes 884760
  34.6 1.2 %copy-done.2 = f32[27,4,8,256]{3,2,1,0:T(8,128)S(1)} copy-done((f32[27,4,8,256]{3,2,1,0:T(8,128)S(1)}, f32[27,4,8,256]{3,2,1,0:T(8,128)}, u32[]{:S(2)}) %copy-start.2) | copy-done | bytes 884760
  35.8 2.7 %middle.1 = (f32[27,4,8,256]{3,2,1,0:T(8,128)}, f32[2,9,8,256]{3,2,1,0:T(8,128)}, f32[40,256]{1,0:T(8,128)}, f32[40,256]{1,0:T(8,128)}, f32[2,8,256]{2,1,0:T(8,128)}, /*index=5*/f32[2,8,256]{2,1,0:T(8,128)}) custom-call(f32[27,4,8,256]{3,2,1,0:T(8,128)S(1)} %copy-done.2, f32[2,9,8,256]{3,2,1,0:T(8,128)S(1)} %collective-permute-done.5.refs_1_, ...), custom_call_target="tpu_custom_call" | custom-call | tf_op jit(solution)/shard_map/middle/pallas_call | solution.py:399
  39.4 3.3 %collective-permute-start.13 = (f32[2,8,256]{2,1,0:T(8,128)}, f32[2,8,256]{2,1,0:T(8,128)S(1)}, u32[]{:S(2)}, u32[]{:S(2)}) collective-permute-start(f32[2,8,256]{2,1,0:T(8,128)} %get-tuple-element.41), channel_id=1, source_target_pairs={{0,9},{1,10},{2,11},{3,12},{4,13},{5,14},{6,15},{7,0},{8,1},{9,2},... | collective-permute-start | bytes 49160 | tf_op jit(solution)/shard_map/ppermute | solution.py:318
  42.8 1.2 %collective-permute-start.14 = (f32[2,8,256]{2,1,0:T(8,128)}, f32[2,8,256]{2,1,0:T(8,128)S(1)}, u32[]{:S(2)}, u32[]{:S(2)}) collective-permute-start(f32[2,8,256]{2,1,0:T(8,128)} %get-tuple-element.42), channel_id=1, source_target_pairs={{0,7},{1,8},{2,9},{3,10},{4,11},{5,12},{6,13},{7,14},{8,15},{9,0},... | collective-permute-start | bytes 49160 | tf_op jit(solution)/shard_map/ppermute | solution.py:318
  44.0 5.4 %collective-permute-done.13.refs_4_ = f32[2,8,256]{2,1,0:T(8,128)S(1)} collective-permute-done((f32[2,8,256]{2,1,0:T(8,128)}, f32[2,8,256]{2,1,0:T(8,128)S(1)}, u32[]{:S(2)}, u32[]{:S(2)}) %collective-permute-start.13) | collective-permute-done | bytes 16416 | tf_op jit(solution)/shard_map/ppermute | solution.py:318
  49.3 0.9 %collective-permute-done.14.refs_5_ = f32[2,8,256]{2,1,0:T(8,128)S(1)} collective-permute-done((f32[2,8,256]{2,1,0:T(8,128)}, f32[2,8,256]{2,1,0:T(8,128)S(1)}, u32[]{:S(2)}, u32[]{:S(2)}) %collective-permute-start.14) | collective-permute-done | bytes 16416 | tf_op jit(solution)/shard_map/ppermute | solution.py:318
  50.3 1.2 %copy-done.3 = f32[27,4,8,256]{3,2,1,0:T(8,128)S(1)} copy-done((f32[27,4,8,256]{3,2,1,0:T(8,128)S(1)}, f32[27,4,8,256]{3,2,1,0:T(8,128)}, u32[]{:S(2)}) %copy-start.3) | copy-done | bytes 884760
  51.4 2.4 %last.1 = f32[27,4,8,256]{3,2,1,0:T(8,128)} custom-call(f32[27,4,8,256]{3,2,1,0:T(8,128)S(1)} %copy-done.3, f32[2,9,8,256]{3,2,1,0:T(8,128)S(1)} %collective-permute-done.10.refs_1_, f32[40,256]{1,0:T(8,128)S(1)} %collective-permute-done.11.refs_2_, f32[40,256]{1,0:T(8,128)S(1)} %collective-permute-done.12.refs_3_, ...), custom_call_target="tpu_custom_call" | custom-call | tf_op jit(solution)/shard_map/last/pallas_call | solution.py:408
  (23 shorter events, 1.6 us)
Async XLA Ops:
  2.7 14.8 %collective-permute-start = (f32[2,11,8,256]{3,2,1,0:T(8,128)}, f32[2,11,8,256]{3,2,1,0:T(8,128)S(1)}, u32[]{:S(2)}, u32[]{:S(2)}) collective-permute-start(f32[2,11,8,256]{3,2,1,0:T(8,128)} %get-tuple-element.25), channel_id=1, source_target_pairs={{0,8},{1,9},{2,10},{3,11},{4,12},{5,13},{6,14},{7,15},{8,0},{9,1},... | collective-permute-start | bytes 540680 | tf_op jit(solution)/shard_map/ppermute | solution.py:318
  5.8 11.7 %collective-permute-start.1 = (f32[48,256]{1,0:T(8,128)}, f32[48,256]{1,0:T(8,128)S(1)}, u32[]{:S(2)}, u32[]{:S(2)}) collective-permute-start(f32[48,256]{1,0:T(8,128)} %get-tuple-element.26), channel_id=1, source_target_pairs={{0,1},{1,2},{2,3},{3,4},{4,5},{5,6},{6,7},{7,8},{8,9},{9,10},{10,1... | collective-permute-start | bytes 147464 | tf_op jit(solution)/shard_map/ppermute | solution.py:318
  7.9 9.6 %collective-permute-start.2 = (f32[48,256]{1,0:T(8,128)}, f32[48,256]{1,0:T(8,128)S(1)}, u32[]{:S(2)}, u32[]{:S(2)}) collective-permute-start(f32[48,256]{1,0:T(8,128)} %get-tuple-element.27), channel_id=1, source_target_pairs={{0,15},{1,0},{2,1},{3,2},{4,3},{5,4},{6,5},{7,6},{8,7},{9,8},{10,9... | collective-permute-start | bytes 147464 | tf_op jit(solution)/shard_map/ppermute | solution.py:318
  7.9 8.4 %collective-permute-start.3 = (f32[2,8,256]{2,1,0:T(8,128)}, f32[2,8,256]{2,1,0:T(8,128)S(1)}, u32[]{:S(2)}, u32[]{:S(2)}) collective-permute-start(f32[2,8,256]{2,1,0:T(8,128)} %get-tuple-element.28), channel_id=1, source_target_pairs={{0,9},{1,10},{2,11},{3,12},{4,13},{5,14},{6,15},{7,0},{8,1},{9,2},... | collective-permute-start | bytes 49160 | tf_op jit(solution)/shard_map/ppermute | solution.py:318
  9.4 8.1 %collective-permute-start.4 = (f32[2,8,256]{2,1,0:T(8,128)}, f32[2,8,256]{2,1,0:T(8,128)S(1)}, u32[]{:S(2)}, u32[]{:S(2)}) collective-permute-start(f32[2,8,256]{2,1,0:T(8,128)} %get-tuple-element.29), channel_id=1, source_target_pairs={{0,7},{1,8},{2,9},{3,10},{4,11},{5,12},{6,13},{7,14},{8,15},{9,0},... | collective-permute-start | bytes 49160 | tf_op jit(solution)/shard_map/ppermute | solution.py:318
  10.5 0.7 %copy-start.5 = (f32[8,3]{0,1:T(4,128)S(1)}, f32[8,3]{0,1:T(4,128)}, u32[]{:S(2)}) copy-start(f32[8,3]{0,1:T(4,128)} %param.8) | copy-start | bytes 292
  17.5 1.2 %copy-start.4 = (f32[27,4,8,256]{3,2,1,0:T(8,128)S(1)}, f32[27,4,8,256]{3,2,1,0:T(8,128)}, u32[]{:S(2)}) copy-start(f32[27,4,8,256]{3,2,1,0:T(8,128)} %get-tuple-element.24.refs_0_) | copy-start | bytes 2654212
  21.8 11.6 %collective-permute-start.5 = (f32[2,9,8,256]{3,2,1,0:T(8,128)}, f32[2,9,8,256]{3,2,1,0:T(8,128)S(1)}, u32[]{:S(2)}, u32[]{:S(2)}) collective-permute-start(f32[2,9,8,256]{3,2,1,0:T(8,128)} %get-tuple-element.31), channel_id=1, source_target_pairs={{0,8},{1,9},{2,10},{3,11},{4,12},{5,13},{6,14},{7,15},{8,0},{9,1},... | collective-permute-start | bytes 442376 | tf_op jit(solution)/shard_map/ppermute | solution.py:318
  21.8 11.6 %collective-permute-start.6 = (f32[40,256]{1,0:T(8,128)}, f32[40,256]{1,0:T(8,128)S(1)}, u32[]{:S(2)}, u32[]{:S(2)}) collective-permute-start(f32[40,256]{1,0:T(8,128)} %get-tuple-element.32), channel_id=1, source_target_pairs={{0,1},{1,2},{2,3},{3,4},{4,5},{5,6},{6,7},{7,8},{8,9},{9,10},{10,1... | collective-permute-start | bytes 122888 | tf_op jit(solution)/shard_map/ppermute | solution.py:318
  22.3 11.1 %collective-permute-start.7 = (f32[40,256]{1,0:T(8,128)}, f32[40,256]{1,0:T(8,128)S(1)}, u32[]{:S(2)}, u32[]{:S(2)}) collective-permute-start(f32[40,256]{1,0:T(8,128)} %get-tuple-element.33), channel_id=1, source_target_pairs={{0,15},{1,0},{2,1},{3,2},{4,3},{5,4},{6,5},{7,6},{8,7},{9,8},{10,9... | collective-permute-start | bytes 122888 | tf_op jit(solution)/shard_map/ppermute | solution.py:318
  24.9 8.5 %collective-permute-start.8 = (f32[2,8,256]{2,1,0:T(8,128)}, f32[2,8,256]{2,1,0:T(8,128)S(1)}, u32[]{:S(2)}, u32[]{:S(2)}) collective-permute-start(f32[2,8,256]{2,1,0:T(8,128)} %get-tuple-element.34), channel_id=1, source_target_pairs={{0,9},{1,10},{2,11},{3,12},{4,13},{5,14},{6,15},{7,0},{8,1},{9,2},... | collective-permute-start | bytes 49160 | tf_op jit(solution)/shard_map/ppermute | solution.py:318
  26.4 7.0 %collective-permute-start.9 = (f32[2,8,256]{2,1,0:T(8,128)}, f32[2,8,256]{2,1,0:T(8,128)S(1)}, u32[]{:S(2)}, u32[]{:S(2)}) collective-permute-start(f32[2,8,256]{2,1,0:T(8,128)} %get-tuple-element.35), channel_id=1, source_target_pairs={{0,7},{1,8},{2,9},{3,10},{4,11},{5,12},{6,13},{7,14},{8,15},{9,0},... | collective-permute-start | bytes 49160 | tf_op jit(solution)/shard_map/ppermute | solution.py:318
  33.4 1.2 %copy-start = (f32[27,4,8,256]{3,2,1,0:T(8,128)S(1)}, f32[27,4,8,256]{3,2,1,0:T(8,128)}, u32[]{:S(2)}) copy-start(f32[27,4,8,256]{3,2,1,0:T(8,128)} %get-tuple-element.36.refs_6_) | copy-start | bytes 2654212
  34.6 1.2 %copy-start.2 = (f32[27,4,8,256]{3,2,1,0:T(8,128)S(1)}, f32[27,4,8,256]{3,2,1,0:T(8,128)}, u32[]{:S(2)}) copy-start(f32[27,4,8,256]{3,2,1,0:T(8,128)} %get-tuple-element.30.refs_0_) | copy-start | bytes 2654212
  35.8 14.5 %copy-start.1 = (f32[27,4,8,256]{3,2,1,0:T(8,128)S(1)}, f32[27,4,8,256]{3,2,1,0:T(8,128)}, u32[]{:S(2)}) copy-start(f32[27,4,8,256]{3,2,1,0:T(8,128)} %get-tuple-element.36.refs_6_) | copy-start | bytes 2654212
  38.4 11.8 %collective-permute-start.10 = (f32[2,9,8,256]{3,2,1,0:T(8,128)}, f32[2,9,8,256]{3,2,1,0:T(8,128)S(1)}, u32[]{:S(2)}, u32[]{:S(2)}) collective-permute-start(f32[2,9,8,256]{3,2,1,0:T(8,128)} %get-tuple-element.38), channel_id=1, source_target_pairs={{0,8},{1,9},{2,10},{3,11},{4,12},{5,13},{6,14},{7,15},{8,0},{9,1},... | collective-permute-start | bytes 442376 | tf_op jit(solution)/shard_map/ppermute | solution.py:318
  38.8 11.5 %collective-permute-start.11 = (f32[40,256]{1,0:T(8,128)}, f32[40,256]{1,0:T(8,128)S(1)}, u32[]{:S(2)}, u32[]{:S(2)}) collective-permute-start(f32[40,256]{1,0:T(8,128)} %get-tuple-element.39), channel_id=1, source_target_pairs={{0,1},{1,2},{2,3},{3,4},{4,5},{5,6},{6,7},{7,8},{8,9},{9,10},{10,1... | collective-permute-start | bytes 122888 | tf_op jit(solution)/shard_map/ppermute | solution.py:318
  38.8 11.5 %collective-permute-start.12 = (f32[40,256]{1,0:T(8,128)}, f32[40,256]{1,0:T(8,128)S(1)}, u32[]{:S(2)}, u32[]{:S(2)}) collective-permute-start(f32[40,256]{1,0:T(8,128)} %get-tuple-element.40), channel_id=1, source_target_pairs={{0,15},{1,0},{2,1},{3,2},{4,3},{5,4},{6,5},{7,6},{8,7},{9,8},{10,9... | collective-permute-start | bytes 122888 | tf_op jit(solution)/shard_map/ppermute | solution.py:318
  39.4 9.9 %collective-permute-start.13 = (f32[2,8,256]{2,1,0:T(8,128)}, f32[2,8,256]{2,1,0:T(8,128)S(1)}, u32[]{:S(2)}, u32[]{:S(2)}) collective-permute-start(f32[2,8,256]{2,1,0:T(8,128)} %get-tuple-element.41), channel_id=1, source_target_pairs={{0,9},{1,10},{2,11},{3,12},{4,13},{5,14},{6,15},{7,0},{8,1},{9,2},... | collective-permute-start | bytes 49160 | tf_op jit(solution)/shard_map/ppermute | solution.py:318
  42.8 7.5 %collective-permute-start.14 = (f32[2,8,256]{2,1,0:T(8,128)}, f32[2,8,256]{2,1,0:T(8,128)S(1)}, u32[]{:S(2)}, u32[]{:S(2)}) collective-permute-start(f32[2,8,256]{2,1,0:T(8,128)} %get-tuple-element.42), channel_id=1, source_target_pairs={{0,7},{1,8},{2,9},{3,10},{4,11},{5,12},{6,13},{7,14},{8,15},{9,0},... | collective-permute-start | bytes 49160 | tf_op jit(solution)/shard_map/ppermute | solution.py:318
  50.3 1.2 %copy-start.3 = (f32[27,4,8,256]{3,2,1,0:T(8,128)S(1)}, f32[27,4,8,256]{3,2,1,0:T(8,128)}, u32[]{:S(2)}) copy-start(f32[27,4,8,256]{3,2,1,0:T(8,128)} %get-tuple-element.37.refs_0_) | copy-start | bytes 2654212
